TPU v7x, 32 devices: a whole 2x2x4 slice. The times are simulated.
32 devices in a mesh: fx: 4 (over z), fy: 4 (over x, core), fz: 2 (over y).
Axes of the slice: x: 2, y: 2, z: 4, core: 2. Of those that a mesh axis runs over, the one named last changes fastest.
Arguments:
- pressure: float32 [128, 512, 256], P('fx', 'fy', 'fz'), may hold values from -6 to 6
- source: float32 [128, 512, 256], P('fx', 'fy', 'fz'), may hold values from -6 to 6
- diag_shift: float32 [128, 512, 256], P('fx', 'fy', 'fz'), may hold values from 0.1 to 2
- iface_cells: int32 [262144], P(('fx', 'fy', 'fz')), may hold values from 0 to 524287
- iface_coef: float32 [262144], P(('fx', 'fy', 'fz')), may hold values from -6 to 6
- iface_xyz: float32 [3, 262144], P(None, ('fx', 'fy', 'fz')), may hold values from -6 to 6
- node_xyz: float32 [3, 65536], P(None, ('fx', 'fy', 'fz')), may hold values from -6 to 6
- owners: int32 [2048], P(('fx', 'fy', 'fz')), may hold values from 0 to 31, as said below
- node_lists: int32 [65536, 8], P(('fx', 'fy', 'fz')), may hold values from 0 to 1048575
Outputs:
- new_pressure: float32 [128, 512, 256], P('fx', 'fy', 'fz')
- node_loads: float32 [65536], P(('fx', 'fy', 'fz'))
Inputs may be any that keep to these rules, and one draw needn't show every extreme that they name: `owners`: among the 64 tiles of one device, at most 4 have the same owner; one device owns exactly 4 tiles of every device's block; every device owns at least one tile.
All inputs are finite; a program needn't handle non-finite values.
Results may differ from a plain program's by a relative error of at most 0.0003.
Values sent between devices are 32-bit elements; how exact they have to be, the bound alone decides.
No kernel may reach another device: no remote copies, remote signals or barrier semaphores. Data moves between devices by JAX's collectives and lax.ppermute only.
A program may use at most 192 MiB of HBM per device.

v0:
```python
import jax
import jax.numpy as jnp
from jax import lax
from jax.sharding import PartitionSpec as P

ITERS = 4
CAP = 4


GAUSS_RATE = 0.5


def extended(cells, sides, width):
    for axis, dim in sides:
        count = lax.axis_size(axis)
        head = lax.slice_in_dim(cells, 0, width, axis=dim)
        tail = lax.slice_in_dim(cells, cells.shape[dim] - width, cells.shape[dim], axis=dim)
        cells = jnp.concatenate(
            [
                lax.ppermute(tail, axis, [(i, (i + 1) % count) for i in range(count)]),
                cells,
                lax.ppermute(head, axis, [((i + 1) % count, i) for i in range(count)]),
            ],
            axis=dim,
        )
    return cells


def face_sweep(field, source, diag_shift):
    edge_x = jnp.stack([field[0], field[-1]], axis=0)
    edge_y = jnp.stack([field[:, 0], field[:, -1]], axis=1)
    edge_z = jnp.stack([field[:, :, 0], field[:, :, -1]], axis=2)
    halo_x = extended(edge_x, (("fx", 0),), 1)
    halo_y = extended(edge_y, (("fy", 1),), 1)
    halo_z = extended(edge_z, (("fz", 2),), 1)
    index_x = lax.broadcasted_iota(jnp.int32, field.shape, 0)
    index_y = lax.broadcasted_iota(jnp.int32, field.shape, 1)
    index_z = lax.broadcasted_iota(jnp.int32, field.shape, 2)
    last_x = field.shape[0] - 1
    last_y = field.shape[1] - 1
    last_z = field.shape[2] - 1
    neighbours = jnp.where(index_x == 0, halo_x[0][None, :, :], jnp.roll(field, 1, 0))
    neighbours = neighbours + jnp.where(
        index_x == last_x, halo_x[3][None, :, :], jnp.roll(field, -1, 0)
    )
    neighbours = neighbours + jnp.where(
        index_y == 0, halo_y[:, 0][:, None, :], jnp.roll(field, 1, 1)
    )
    neighbours = neighbours + jnp.where(
        index_y == last_y, halo_y[:, 3][:, None, :], jnp.roll(field, -1, 1)
    )
    neighbours = neighbours + jnp.where(
        index_z == 0, halo_z[:, :, 0][:, :, None], jnp.roll(field, 1, 2)
    )
    neighbours = neighbours + jnp.where(
        index_z == last_z, halo_z[:, :, 3][:, :, None], jnp.roll(field, -1, 2)
    )
    return (neighbours + source) / (6.0 + diag_shift)


def on_device(
    pressure, source, diag_shift, iface_cells, iface_coef, iface_xyz, node_xyz, owners, node_lists
):
    devices = lax.axis_size(("fx", "fy", "fz"))
    tiles_dev = owners.shape[0]
    tile_width = iface_coef.shape[0] // tiles_dev
    node_count = node_lists.shape[0]
    neigh_count = node_lists.shape[1]
    lane_width = pressure.shape[2]
    row_table = pressure.reshape(-1, lane_width)
    fetched = row_table[iface_cells // lane_width]
    lane_pick = (iface_cells % lane_width)[:, None] == lax.broadcasted_iota(
        jnp.int32, (1, lane_width), 1
    )
    at_cells = jnp.sum(jnp.where(lane_pick, fetched, 0.0), axis=1)
    values = iface_coef * at_cells
    payload = jnp.concatenate(
        [
            values.reshape(tiles_dev, 1, tile_width),
            iface_xyz.reshape(3, tiles_dev, tile_width).transpose(1, 0, 2),
        ],
        axis=1,
    )
    payload = payload.reshape(tiles_dev, 4 * tile_width)
    owned_by = (owners[:, None] == jnp.arange(devices, dtype=jnp.int32)[None, :]).astype(jnp.int32)
    earlier = jnp.cumsum(owned_by, axis=0) - owned_by
    order_rank = jnp.sum(earlier * owned_by, axis=1)
    target = owners * CAP + order_rank
    placing = (target[None, :] == jnp.arange(devices * CAP, dtype=jnp.int32)[:, None]).astype(
        jnp.float32
    )
    outgoing = jnp.dot(
        placing, payload, precision=lax.Precision.HIGHEST, preferred_element_type=jnp.float32
    )
    outgoing = outgoing.reshape(devices * CAP, 4, tile_width)
    filled = jnp.sum(placing, axis=1)
    incoming, arrived = (
        lax.all_to_all(outgoing, ("fx", "fy", "fz"), split_axis=0, concat_axis=0, tiled=True),
        lax.all_to_all(filled, ("fx", "fy", "fz"), split_axis=0, concat_axis=0, tiled=True),
    )
    arrived_int = arrived.astype(jnp.int32)
    prefix = jnp.cumsum(arrived_int)
    owned_count = prefix[-1]
    wanted = (node_lists % owned_count).reshape(node_count * neigh_count)
    selector = ((prefix[None, :] == wanted[:, None] + 1) & (arrived_int[None, :] > 0)).astype(
        jnp.float32
    )
    picked = jnp.dot(
        selector,
        incoming.reshape(devices * CAP, 4 * tile_width),
        precision=lax.Precision.HIGHEST,
        preferred_element_type=jnp.float32,
    )
    picked = picked.reshape(node_count, neigh_count, 4, tile_width)
    distance = jnp.zeros((node_count, neigh_count, tile_width), jnp.float32)
    for component in range(3):
        gap_axis = node_xyz[component][:, None, None] - picked[:, :, component + 1, :]
        distance = distance + gap_axis * gap_axis
    node_loads = jnp.sum(jnp.exp(-GAUSS_RATE * distance) * picked[:, :, 0, :], axis=(1, 2))
    pressure_now = pressure
    for sweep_index in range(ITERS):
        pressure_now = face_sweep(pressure_now, source, diag_shift)
    return (pressure_now, node_loads)


def solution(mesh):
    placed = (
        P("fx", "fy", "fz"),
        P("fx", "fy", "fz"),
        P("fx", "fy", "fz"),
        P(("fx", "fy", "fz")),
        P(("fx", "fy", "fz")),
        P(None, ("fx", "fy", "fz")),
        P(None, ("fx", "fy", "fz")),
        P(("fx", "fy", "fz")),
        P(("fx", "fy", "fz"), None),
    )
    return jax.shard_map(
        on_device,
        mesh=mesh,
        in_specs=placed,
        out_specs=(P("fx", "fy", "fz"), P(("fx", "fy", "fz"))),
        check_vma=False,
    )
```

profile of v0, /device:TPU:0, one launch (start us, length us, event | category | flops | bytes accessed | tf_op | source)
XLA Modules:
  0.0 251.7 jit_solution(13367614697641180582)
XLA Ops:
  0.6 4.9 %fusion.78 = (f32[32,128,1]{2,1,0:T(8,128)}, f32[32,128,1]{2,1,0:T(8,128)}) fusion(f32[32,128,128]{2,1,0:T(8,128)} %param.9), kind=kLoop, calls=%fused_computation.130 | loop fusion | bytes 65536 | tf_op jit(solution)/shard_map/slice | solution.py:32
  5.6 2.4 copy.133
  7.9 3.0 %collective-permute-start.4 = (f32[32,128,1]{1,0,2:T(8,128)S(1)}, f32[32,128,1]{1,0,2:T(8,128)S(1)}, u32[]{:S(2)}, u32[]{:S(2)}) collective-permute-start(f32[32,128,1]{1,0,2:T(8,128)S(1)} %copy.133), channel_id=1, source_target_pairs={{0,1},{1,0},{2,3},{3,2},{4,5},{5,4},{6,7},{7,6},{8,9},{9,8},{10,11... | collective-permute-start | bytes 49160 | tf_op jit(solution)/shard_map/ppermute | solution.py:20
  11.0 2.2 copy.135
  13.2 2.1 collective-permute-start
  15.4 2.1 collective-permute-start.1
  18.0 0.7 all_to_all.9
  18.7 4.5 %all-to-all-start = ((f32[32,4,1]{1,2,0:T(1,128)}), f32[32,4,1]{1,2,0:T(1,128)S(1)}, u32[]{:S(2)}, u32[]{:S(2)}) async-start(f32[32,4,1]{1,2,0:T(1,128)} %bitcast.25), calls=%async_computation | async-start | bytes 32768 | tf_op jit(solution)/shard_map/all_to_all | solution.py:99
  23.2 2.8 %fusion.77 = (f32[32,128,127]{2,1,0:T(8,128)}, f32[32,128,127]{2,1,0:T(8,128)}) fusion(f32[32,128,128]{2,1,0:T(8,128)S(1)} %copy-done), kind=kLoop, calls=%fused_computation.129 | loop fusion | bytes 8323072 | tf_op jit(solution)/shard_map/jit(_roll_static)/slice | solution.py:56
  26.0 2.4 fusion.79
  28.4 2.4 fusion.81
  30.8 27.9 %gather_fusion = f32[8192,128]{1,0:T(8,128)} fusion(f32[4096,128]{1,0:T(8,128)S(1)} %bitcast.112, s32[8192]{0:T(1024)S(1)} %get-tuple-element.60), kind=kCustom, calls=%fused_computation | custom fusion | bytes 8421376 | tf_op jit(solution)/shard_map/gather | solution.py:71
  58.8 4.9 %select_reduce_fusion = f32[8192]{0:T(1024)S(1)} fusion(f32[8192,128]{1,0:T(8,128)} %gather_fusion, s32[8192]{0:T(1024)S(1)} %get-tuple-element.59), kind=kLoop, calls=%fused_computation.21 | loop fusion | flops 3137536 | bytes 4259840 | tf_op jit(solution)/shard_map/reduce_sum | solution.py:75
  64.2 2.6 %copy.92 = f32[32,128,1]{2,0,1:T(8,128)} copy(f32[32,128,1]{2,1,0:T(8,128)S(1)} %copy-done.2) | data formatting | bytes 32768 | tf_op jit(solution)/shard_map/slice | solution.py:32
  66.8 2.5 %copy.96 = f32[32,128,1]{2,0,1:T(8,128)} copy(f32[32,128,1]{2,1,0:T(8,128)S(1)} %copy-done.1) | data formatting | bytes 32768 | tf_op jit(solution)/shard_map/slice | solution.py:32
  69.3 2.6 %copy.134 = f32[32,128,127]{2,0,1:T(8,128)} copy(f32[32,128,127]{2,1,0:T(8,128)S(1)} %copy-done.6) | data formatting | bytes 4161536
  72.0 2.6 %copy.136 = f32[32,128,127]{2,0,1:T(8,128)} copy(f32[32,128,127]{2,1,0:T(8,128)S(1)} %copy-done.5) | data formatting | bytes 4161536
  74.5 2.6 %copy.130 = f32[32,127,128]{2,0,1:T(8,128)} copy(f32[32,127,128]{2,1,0:T(8,128)S(1)} %copy-done.4) | data formatting | bytes 4161536
  77.1 2.5 copy.132
  79.6 2.5 copy.126
  82.1 2.6 %copy.128 = f32[31,128,128]{2,0,1:T(8,128)} copy(f32[31,128,128]{2,1,0:T(8,128)S(1)} %copy-done.7) | data formatting | bytes 4063232
  84.7 0.9 copy.118
  85.6 5.8 %all-to-all-start.1 = ((f32[128,4,128]{2,1,0:T(4,128)}), f32[128,4,128]{2,1,0:T(4,128)S(1)}, u32[]{:S(2)}, u32[]{:S(2)}) async-start(f32[128,4,128]{2,1,0:T(4,128)} %copy.118), calls=%async_computation.1 | async-start | bytes 524288 | tf_op jit(solution)/shard_map/all_to_all | solution.py:98
  93.6 0.7 fusion.51
  94.3 2.1 collective-permute-start.3
  96.8 0.9 collective-permute-done.3
  97.8 11.7 %fusion.25 = f32[32,128,128]{2,0,1:T(8,128)S(1)} fusion(f32[31,128,128]{2,0,1:T(8,128)} %copy.126, f32[1,128,128]{2,0,1:T(1,128)S(1)} %bitcast.117, f32[1,128,128]{2,0,1:T(1,128)S(1)} %bitcast.115, f32[31,128,128]{2,0,1:T(8,128)} %copy.128, f32[32,127,128]{2,0,1:T(8,128)} %copy.130, f32[32,1,128]{2,0,1:T(8,128)S(1)} %bitcast.131, ...), kind=kLoop, calls=%fused_computation.33 | loop fusion | flops 10485760 | bytes 19071296 | tf_op jit(solution)/shard_map/div | solution.py:58
  109.5 2.8 %fusion.72 = (f32[32,128,1]{2,0,1:T(8,128)}, f32[32,128,1]{2,0,1:T(8,128)}) fusion(f32[32,128,128]{2,0,1:T(8,128)S(1)} %fusion.25), kind=kLoop, calls=%fused_computation.124 | loop fusion | bytes 65536 | tf_op jit(solution)/shard_map/slice | solution.py:32
  112.3 2.8 %fusion.71 = (f32[32,128,127]{2,0,1:T(8,128)}, f32[32,128,127]{2,0,1:T(8,128)}) fusion(f32[32,128,128]{2,0,1:T(8,128)S(1)} %fusion.25), kind=kLoop, calls=%fused_computation.123 | loop fusion | bytes 8323072 | tf_op jit(solution)/shard_map/jit(_roll_static)/slice | solution.py:56
  115.1 2.6 %fusion.75 = (f32[31,128,128]{2,0,1:T(8,128)}, f32[31,128,128]{2,0,1:T(8,128)}) fusion(f32[32,128,128]{2,0,1:T(8,128)S(1)} %fusion.25), kind=kLoop, calls=%fused_computation.127 | loop fusion | bytes 8126464 | tf_op jit(solution)/shard_map/jit(_roll_static)/slice | solution.py:44
  117.8 2.7 %copy.99 = f32[32,128,1]{1,0,2:T(8,128)S(1)} copy(f32[32,128,1]{2,0,1:T(8,128)} %get-tuple-element.35) | data formatting | bytes 32768 | tf_op jit(solution)/shard_map/slice | solution.py:32
  120.4 1.5 collective-permute-start.10
  121.9 2.7 %copy.101 = f32[32,128,1]{1,0,2:T(8,128)S(1)} copy(f32[32,128,1]{2,0,1:T(8,128)} %get-tuple-element.34) | data formatting | bytes 32768 | tf_op jit(solution)/shard_map/slice | solution.py:32
  124.6 0.6 collective-permute-start.11
  125.2 1.5 collective-permute-start.6
  126.6 2.4 collective-permute-start.7
  129.0 1.9 collective-permute-start.9
  130.9 2.7 %fusion.73 = (f32[32,127,128]{2,0,1:T(8,128)}, f32[32,127,128]{2,0,1:T(8,128)}) fusion(f32[32,128,128]{2,0,1:T(8,128)S(1)} %fusion.25), kind=kLoop, calls=%fused_computation.125 | loop fusion | bytes 8323072 | tf_op jit(solution)/shard_map/jit(_roll_static)/slice | solution.py:50
  133.8 11.7 %fusion.32 = f32[32,128,128]{2,0,1:T(8,128)S(1)} fusion(f32[31,128,128]{2,0,1:T(8,128)} %get-tuple-element.41, f32[1,128,128]{2,0,1:T(1,128)S(1)} %get-tuple-element.43, f32[1,128,128]{2,0,1:T(1,128)S(1)} %get-tuple-element.42, f32[31,128,128]{2,0,1:T(8,128)} %get-tuple-element.40, f32[32,127,128]{2,0,1:T(8,128)} %get-tuple-element.37, ...), kind=kLoop, calls=%fused_computation.46 | loop fusion | flops 10485760 | bytes 19071296 | tf_op jit(solution)/shard_map/div | solution.py:58
  145.6 2.8 %fusion.66 = (f32[32,128,1]{2,0,1:T(8,128)}, f32[32,128,1]{2,0,1:T(8,128)}) fusion(f32[32,128,128]{2,0,1:T(8,128)S(1)} %fusion.32), kind=kLoop, calls=%fused_computation.118 | loop fusion | bytes 65536 | tf_op jit(solution)/shard_map/slice | solution.py:32
  148.3 2.8 %fusion.65 = (f32[32,128,127]{2,0,1:T(8,128)}, f32[32,128,127]{2,0,1:T(8,128)}) fusion(f32[32,128,128]{2,0,1:T(8,128)S(1)} %fusion.32), kind=kLoop, calls=%fused_computation.117 | loop fusion | bytes 8323072 | tf_op jit(solution)/shard_map/jit(_roll_static)/slice | solution.py:56
  151.1 2.6 %fusion.69 = (f32[31,128,128]{2,0,1:T(8,128)}, f32[31,128,128]{2,0,1:T(8,128)}) fusion(f32[32,128,128]{2,0,1:T(8,128)S(1)} %fusion.32), kind=kLoop, calls=%fused_computation.121 | loop fusion | bytes 8126464 | tf_op jit(solution)/shard_map/jit(_roll_static)/slice | solution.py:44
  153.8 2.7 %copy.104 = f32[32,128,1]{1,0,2:T(8,128)S(1)} copy(f32[32,128,1]{2,0,1:T(8,128)} %get-tuple-element.23) | data formatting | bytes 32768 | tf_op jit(solution)/shard_map/slice | solution.py:32
  156.5 1.5 collective-permute-start.16
  158.0 2.7 %copy.106 = f32[32,128,1]{1,0,2:T(8,128)S(1)} copy(f32[32,128,1]{2,0,1:T(8,128)} %get-tuple-element.22) | data formatting | bytes 32768 | tf_op jit(solution)/shard_map/slice | solution.py:32
  160.6 0.6 collective-permute-start.17
  161.2 3.8 %collective-permute-start.13 = (f32[1,128,128]{2,0,1:T(1,128)S(1)}, f32[1,128,128]{2,0,1:T(1,128)S(1)}, u32[]{:S(2)}, u32[]{:S(2)}) collective-permute-start(f32[1,128,128]{2,0,1:T(1,128)S(1)} %get-tuple-element.30), channel_id=1, source_target_pairs={{8,0},{16,8},{24,16},{0,24},{9,1},{17,9},{25,17},{1,25},{10,2},{18... | collective-permute-start | bytes 196616 | tf_op jit(solution)/shard_map/ppermute | solution.py:22
  165.1 1.9 collective-permute-start.15
  167.0 2.7 %fusion.67 = (f32[32,127,128]{2,0,1:T(8,128)}, f32[32,127,128]{2,0,1:T(8,128)}) fusion(f32[32,128,128]{2,0,1:T(8,128)S(1)} %fusion.32), kind=kLoop, calls=%fused_computation.119 | loop fusion | bytes 8323072 | tf_op jit(solution)/shard_map/jit(_roll_static)/slice | solution.py:50
  169.9 11.7 %fusion.39 = f32[32,128,128]{2,0,1:T(8,128)S(1)} fusion(f32[31,128,128]{2,0,1:T(8,128)} %get-tuple-element.29, f32[1,128,128]{2,0,1:T(1,128)S(1)} %get-tuple-element.31, f32[1,128,128]{2,0,1:T(1,128)S(1)} %get-tuple-element.30, f32[31,128,128]{2,0,1:T(8,128)} %get-tuple-element.28, f32[32,127,128]{2,0,1:T(8,128)} %get-tuple-element.25, ...), kind=kLoop, calls=%fused_computation.59 | loop fusion | flops 10485760 | bytes 19071296 | tf_op jit(solution)/shard_map/div | solution.py:58
  181.7 2.8 %fusion.60 = (f32[32,128,1]{2,0,1:T(8,128)}, f32[32,128,1]{2,0,1:T(8,128)}) fusion(f32[32,128,128]{2,0,1:T(8,128)S(1)} %fusion.39), kind=kLoop, calls=%fused_computation.112 | loop fusion | bytes 65536 | tf_op jit(solution)/shard_map/slice | solution.py:32
  184.4 2.6 %fusion.63 = (f32[31,128,128]{2,0,1:T(8,128)}, f32[31,128,128]{2,0,1:T(8,128)}) fusion(f32[32,128,128]{2,0,1:T(8,128)S(1)} %fusion.39), kind=kLoop, calls=%fused_computation.115 | loop fusion | bytes 8126464 | tf_op jit(solution)/shard_map/jit(_roll_static)/slice | solution.py:44
  187.1 2.8 %fusion.59 = (f32[32,128,127]{2,0,1:T(8,128)}, f32[32,128,127]{2,0,1:T(8,128)}) fusion(f32[32,128,128]{2,0,1:T(8,128)S(1)} %fusion.39), kind=kLoop, calls=%fused_computation.111 | loop fusion | bytes 8323072 | tf_op jit(solution)/shard_map/jit(_roll_static)/slice | solution.py:56
  190.0 2.7 %copy.109 = f32[32,128,1]{1,0,2:T(8,128)S(1)} copy(f32[32,128,1]{2,0,1:T(8,128)} %get-tuple-element.11) | data formatting | bytes 32768 | tf_op jit(solution)/shard_map/slice | solution.py:32
  192.6 1.5 collective-permute-start.22
  194.1 2.7 %copy.111 = f32[32,128,1]{1,0,2:T(8,128)S(1)} copy(f32[32,128,1]{2,0,1:T(8,128)} %get-tuple-element.10) | data formatting | bytes 32768 | tf_op jit(solution)/shard_map/slice | solution.py:32
  196.8 0.6 collective-permute-start.23
  197.4 3.8 %collective-permute-start.19 = (f32[1,128,128]{2,0,1:T(1,128)S(1)}, f32[1,128,128]{2,0,1:T(1,128)S(1)}, u32[]{:S(2)}, u32[]{:S(2)}) collective-permute-start(f32[1,128,128]{2,0,1:T(1,128)S(1)} %get-tuple-element.18), channel_id=1, source_target_pairs={{8,0},{16,8},{24,16},{0,24},{9,1},{17,9},{25,17},{1,25},{10,2},{18... | collective-permute-start | bytes 196616 | tf_op jit(solution)/shard_map/ppermute | solution.py:22
  201.2 2.0 collective-permute-start.21
  203.2 2.7 %fusion.61 = (f32[32,127,128]{2,0,1:T(8,128)}, f32[32,127,128]{2,0,1:T(8,128)}) fusion(f32[32,128,128]{2,0,1:T(8,128)S(1)} %fusion.39), kind=kLoop, calls=%fused_computation.113 | loop fusion | bytes 8323072 | tf_op jit(solution)/shard_map/jit(_roll_static)/slice | solution.py:50
  206.1 11.7 %fusion.46 = f32[32,128,128]{2,0,1:T(8,128)S(1)} fusion(f32[31,128,128]{2,0,1:T(8,128)} %get-tuple-element.17, f32[1,128,128]{2,0,1:T(1,128)S(1)} %get-tuple-element.19, f32[1,128,128]{2,0,1:T(1,128)S(1)} %get-tuple-element.18, f32[31,128,128]{2,0,1:T(8,128)} %get-tuple-element.16, f32[32,127,128]{2,0,1:T(8,128)} %get-tuple-element.13, ...), kind=kLoop, calls=%fused_computation.72 | loop fusion | flops 10485760 | bytes 19071296 | tf_op jit(solution)/shard_map/div | solution.py:58
  217.8 2.5 %copy.123 = f32[32,128,128]{2,1,0:T(8,128)} copy(f32[32,128,128]{2,0,1:T(8,128)S(1)} %fusion.46) | data formatting | bytes 4194304
  220.5 17.6 %fusion.12 = f32[2048,8,4,128]{0,3,2,1:T(8,128)} fusion(s32[2048,8]{0,1:T(8,128)S(1)} %fusion.51, s32[128]{0:T(128)S(1)} %reduce.1, pred[128]{0:T(512)(128)(4,1)S(1)} %gt.13, f32[128,4,128]{0,2,1:T(8,128)S(1)} %copy.119), kind=kOutput, calls=%fused_computation.17 | convolution fusion | flops 12889096192 | bytes 33882752 | tf_op jit(solution)/shard_map/dot_general | solution.py:108
  238.1 13.4 %fusion.1 = f32[2048]{0:T(1024)} fusion(f32[2048,8,4,128]{0,3,2,1:T(8,128)} %fusion.12, f32[2048]{0:T(1024)S(1)} %bitcast.133, f32[2048]{0:T(1024)S(1)} %bitcast.134, f32[2048]{0:T(1024)S(1)} %bitcast.132), kind=kLoop, calls=%fused_computation.3 | loop fusion | flops 23066624 | bytes 33587200 | tf_op jit(solution)/shard_map/reduce_sum | solution.py:119
  (98 shorter events, 3.5 us)
Async XLA Ops:
  5.6 7.6 %copy-start = (f32[32,128,128]{2,1,0:T(8,128)S(1)}, f32[32,128,128]{2,1,0:T(8,128)}, u32[]{:S(2)}) copy-start(f32[32,128,128]{2,1,0:T(8,128)} %param.9) | copy-start | bytes 6291460
  5.6 12.0 %copy-start.14 = (s32[64]{0:T(128)S(1)}, s32[64]{0:T(128)}, u32[]{:S(2)}) copy-start(s32[64]{0:T(128)} %param.16) | copy-start | bytes 772
  7.9 86.3 %collective-permute-start.4 = (f32[32,128,1]{1,0,2:T(8,128)S(1)}, f32[32,128,1]{1,0,2:T(8,128)S(1)}, u32[]{:S(2)}, u32[]{:S(2)}) collective-permute-start(f32[32,128,1]{1,0,2:T(8,128)S(1)} %copy.133), channel_id=1, source_target_pairs={{0,1},{1,0},{2,3},{3,2},{4,5},{5,4},{6,7},{7,6},{8,9},{9,8},{10,11... | collective-permute-start | bytes 49160 | tf_op jit(solution)/shard_map/ppermute | solution.py:20
  13.2 83.6 %collective-permute-start.5 = (f32[32,128,1]{1,0,2:T(8,128)S(1)}, f32[32,128,1]{1,0,2:T(8,128)S(1)}, u32[]{:S(2)}, u32[]{:S(2)}) collective-permute-start(f32[32,128,1]{1,0,2:T(8,128)S(1)} %copy.135), channel_id=1, source_target_pairs={{1,0},{0,1},{3,2},{2,3},{5,4},{4,5},{7,6},{6,7},{9,8},{8,9},{11,10... | collective-permute-start | bytes 49160 | tf_op jit(solution)/shard_map/ppermute | solution.py:22
  13.2 84.5 %collective-permute-start = (f32[1,128,128]{2,0,1:T(1,128)S(1)}, f32[1,128,128]{2,0,1:T(1,128)S(1)}, u32[]{:S(2)}, u32[]{:S(2)}) collective-permute-start(f32[1,128,128]{2,0,1:T(1,128)S(1)} %bitcast.116), channel_id=1, source_target_pairs={{0,8},{8,16},{16,24},{24,0},{1,9},{9,17},{17,25},{25,1},{2,10},{10... | collective-permute-start | bytes 196616 | tf_op jit(solution)/shard_map/ppermute | solution.py:20
  15.4 82.4 %collective-permute-start.1 = (f32[1,128,128]{2,0,1:T(1,128)S(1)}, f32[1,128,128]{2,0,1:T(1,128)S(1)}, u32[]{:S(2)}, u32[]{:S(2)}) collective-permute-start(f32[1,128,128]{2,0,1:T(1,128)S(1)} %bitcast.114), channel_id=1, source_target_pairs={{8,0},{16,8},{24,16},{0,24},{9,1},{17,9},{25,17},{1,25},{10,2},{18... | collective-permute-start | bytes 196616 | tf_op jit(solution)/shard_map/ppermute | solution.py:22
  17.5 79.4 %collective-permute-start.2 = (f32[32,1,128]{2,0,1:T(8,128)S(1)}, f32[32,1,128]{2,0,1:T(8,128)S(1)}, u32[]{:S(2)}, u32[]{:S(2)}) collective-permute-start(f32[32,1,128]{2,0,1:T(8,128)S(1)} %bitcast.130), channel_id=1, source_target_pairs={{0,2},{2,4},{4,6},{6,0},{1,3},{3,5},{5,7},{7,1},{8,10},{10,12},{12... | collective-permute-start | bytes 49160 | tf_op jit(solution)/shard_map/ppermute | solution.py:20
  18.7 66.9 %all-to-all-start = ((f32[32,4,1]{1,2,0:T(1,128)}), f32[32,4,1]{1,2,0:T(1,128)S(1)}, u32[]{:S(2)}, u32[]{:S(2)}) async-start(f32[32,4,1]{1,2,0:T(1,128)} %bitcast.25), calls=%async_computation | async-start | bytes 32768 | tf_op jit(solution)/shard_map/all_to_all | solution.py:99
  28.4 2.4 copy-start.11
  58.7 4.9 %copy-start.12 = (f32[8192]{0:T(1024)S(1)}, f32[8192]{0:T(1024)}, u32[]{:S(2)}) copy-start(f32[8192]{0:T(1024)} %param.13) | copy-start | bytes 98308
  58.7 4.9 %copy-start.9 = (f32[3,8192]{1,0:T(4,128)S(1)}, f32[3,8192]{1,0:T(4,128)}, u32[]{:S(2)}) copy-start(f32[3,8192]{1,0:T(4,128)} %param.14) | copy-start | bytes 294916
  58.7 5.4 %copy-start.13 = (f32[3,2048]{1,0:T(4,128)S(1)}, f32[3,2048]{1,0:T(4,128)}, u32[]{:S(2)}) copy-start(f32[3,2048]{1,0:T(4,128)} %param.15) | copy-start | bytes 73732
  58.8 5.4 %copy-start.2 = (f32[32,128,1]{2,1,0:T(8,128)S(1)}, f32[32,128,1]{2,1,0:T(8,128)}, u32[]{:S(2)}) copy-start(f32[32,128,1]{2,1,0:T(8,128)} %get-tuple-element.47) | copy-start | bytes 49156
  64.2 2.6 %copy-start.1 = (f32[32,128,1]{2,1,0:T(8,128)S(1)}, f32[32,128,1]{2,1,0:T(8,128)}, u32[]{:S(2)}) copy-start(f32[32,128,1]{2,1,0:T(8,128)} %get-tuple-element.46) | copy-start | bytes 49156
  66.8 2.5 %copy-start.6 = (f32[32,128,127]{2,1,0:T(8,128)S(1)}, f32[32,128,127]{2,1,0:T(8,128)}, u32[]{:S(2)}) copy-start(f32[32,128,127]{2,1,0:T(8,128)} %get-tuple-element.45) | copy-start | bytes 6242308
  69.3 2.6 %copy-start.5 = (f32[32,128,127]{2,1,0:T(8,128)S(1)}, f32[32,128,127]{2,1,0:T(8,128)}, u32[]{:S(2)}) copy-start(f32[32,128,127]{2,1,0:T(8,128)} %get-tuple-element.44) | copy-start | bytes 6242308
  72.0 2.6 %copy-start.4 = (f32[32,127,128]{2,1,0:T(8,128)S(1)}, f32[32,127,128]{2,1,0:T(8,128)}, u32[]{:S(2)}) copy-start(f32[32,127,128]{2,1,0:T(8,128)} %get-tuple-element.49) | copy-start | bytes 6242308
  74.5 2.6 %copy-start.3 = (f32[32,127,128]{2,1,0:T(8,128)S(1)}, f32[32,127,128]{2,1,0:T(8,128)}, u32[]{:S(2)}) copy-start(f32[32,127,128]{2,1,0:T(8,128)} %get-tuple-element.48) | copy-start | bytes 6242308
  77.1 2.5 %copy-start.8 = (f32[31,128,128]{2,1,0:T(8,128)S(1)}, f32[31,128,128]{2,1,0:T(8,128)}, u32[]{:S(2)}) copy-start(f32[31,128,128]{2,1,0:T(8,128)} %get-tuple-element.53) | copy-start | bytes 6094852
  79.6 2.5 copy-start.7
  82.1 11.4 %copy-start.10 = (s32[2048,8]{0,1:T(8,128)S(1)}, s32[2048,8]{0,1:T(8,128)}, u32[]{:S(2)}) copy-start(s32[2048,8]{0,1:T(8,128)} %param.17) | copy-start | bytes 196612
  85.6 134.8 %all-to-all-start.1 = ((f32[128,4,128]{2,1,0:T(4,128)}), f32[128,4,128]{2,1,0:T(4,128)S(1)}, u32[]{:S(2)}, u32[]{:S(2)}) async-start(f32[128,4,128]{2,1,0:T(4,128)} %copy.118), calls=%async_computation.1 | async-start | bytes 524288 | tf_op jit(solution)/shard_map/all_to_all | solution.py:98
  94.3 3.5 %collective-permute-start.3 = (f32[32,1,128]{2,0,1:T(8,128)S(1)}, f32[32,1,128]{2,0,1:T(8,128)S(1)}, u32[]{:S(2)}, u32[]{:S(2)}) collective-permute-start(f32[32,1,128]{2,0,1:T(8,128)S(1)} %bitcast.128), channel_id=1, source_target_pairs={{2,0},{4,2},{6,4},{0,6},{3,1},{5,3},{7,5},{1,7},{10,8},{12,10},{14... | collective-permute-start | bytes 49160 | tf_op jit(solution)/shard_map/ppermute | solution.py:22
  120.4 8.6 %collective-permute-start.10 = (f32[32,128,1]{1,0,2:T(8,128)S(1)}, f32[32,128,1]{1,0,2:T(8,128)S(1)}, u32[]{:S(2)}, u32[]{:S(2)}) collective-permute-start(f32[32,128,1]{1,0,2:T(8,128)S(1)} %copy.99), channel_id=1, source_target_pairs={{0,1},{1,0},{2,3},{3,2},{4,5},{5,4},{6,7},{7,6},{8,9},{9,8},{10,11... | collective-permute-start | bytes 49160 | tf_op jit(solution)/shard_map/ppermute | solution.py:20
  124.6 9.1 %collective-permute-start.11 = (f32[32,128,1]{1,0,2:T(8,128)S(1)}, f32[32,128,1]{1,0,2:T(8,128)S(1)}, u32[]{:S(2)}, u32[]{:S(2)}) collective-permute-start(f32[32,128,1]{1,0,2:T(8,128)S(1)} %copy.101), channel_id=1, source_target_pairs={{1,0},{0,1},{3,2},{2,3},{5,4},{4,5},{7,6},{6,7},{9,8},{8,9},{11,10... | collective-permute-start | bytes 49160 | tf_op jit(solution)/shard_map/ppermute | solution.py:22
  125.2 8.6 %collective-permute-start.6 = (f32[1,128,128]{2,0,1:T(1,128)S(1)}, f32[1,128,128]{2,0,1:T(1,128)S(1)}, u32[]{:S(2)}, u32[]{:S(2)}) collective-permute-start(f32[1,128,128]{2,0,1:T(1,128)S(1)} %get-tuple-element.43), channel_id=1, source_target_pairs={{0,8},{8,16},{16,24},{24,0},{1,9},{9,17},{17,25},{25,1},{2,10},{10... | collective-permute-start | bytes 196616 | tf_op jit(solution)/shard_map/ppermute | solution.py:20
  126.6 7.2 %collective-permute-start.7 = (f32[1,128,128]{2,0,1:T(1,128)S(1)}, f32[1,128,128]{2,0,1:T(1,128)S(1)}, u32[]{:S(2)}, u32[]{:S(2)}) collective-permute-start(f32[1,128,128]{2,0,1:T(1,128)S(1)} %get-tuple-element.42), channel_id=1, source_target_pairs={{8,0},{16,8},{24,16},{0,24},{9,1},{17,9},{25,17},{1,25},{10,2},{18... | collective-permute-start | bytes 196616 | tf_op jit(solution)/shard_map/ppermute | solution.py:22
  129.0 4.8 %collective-permute-start.8 = (f32[32,1,128]{2,0,1:T(8,128)S(1)}, f32[32,1,128]{2,0,1:T(8,128)S(1)}, u32[]{:S(2)}, u32[]{:S(2)}) collective-permute-start(f32[32,1,128]{2,0,1:T(8,128)S(1)} %get-tuple-element.39), channel_id=1, source_target_pairs={{0,2},{2,4},{4,6},{6,0},{1,3},{3,5},{5,7},{7,1},{8,10},{10,12},{12... | collective-permute-start | bytes 49160 | tf_op jit(solution)/shard_map/ppermute | solution.py:20
  129.0 4.8 %collective-permute-start.9 = (f32[32,1,128]{2,0,1:T(8,128)S(1)}, f32[32,1,128]{2,0,1:T(8,128)S(1)}, u32[]{:S(2)}, u32[]{:S(2)}) collective-permute-start(f32[32,1,128]{2,0,1:T(8,128)S(1)} %get-tuple-element.38), channel_id=1, source_target_pairs={{2,0},{4,2},{6,4},{0,6},{3,1},{5,3},{7,5},{1,7},{10,8},{12,10},{14... | collective-permute-start | bytes 49160 | tf_op jit(solution)/shard_map/ppermute | solution.py:22
  156.5 8.6 %collective-permute-start.16 = (f32[32,128,1]{1,0,2:T(8,128)S(1)}, f32[32,128,1]{1,0,2:T(8,128)S(1)}, u32[]{:S(2)}, u32[]{:S(2)}) collective-permute-start(f32[32,128,1]{1,0,2:T(8,128)S(1)} %copy.104), channel_id=1, source_target_pairs={{0,1},{1,0},{2,3},{3,2},{4,5},{5,4},{6,7},{7,6},{8,9},{9,8},{10,11... | collective-permute-start | bytes 49160 | tf_op jit(solution)/shard_map/ppermute | solution.py:20
  160.6 9.2 %collective-permute-start.17 = (f32[32,128,1]{1,0,2:T(8,128)S(1)}, f32[32,128,1]{1,0,2:T(8,128)S(1)}, u32[]{:S(2)}, u32[]{:S(2)}) collective-permute-start(f32[32,128,1]{1,0,2:T(8,128)S(1)} %copy.106), channel_id=1, source_target_pairs={{1,0},{0,1},{3,2},{2,3},{5,4},{4,5},{7,6},{6,7},{9,8},{8,9},{11,10... | collective-permute-start | bytes 49160 | tf_op jit(solution)/shard_map/ppermute | solution.py:22
  161.2 8.7 %collective-permute-start.12 = (f32[1,128,128]{2,0,1:T(1,128)S(1)}, f32[1,128,128]{2,0,1:T(1,128)S(1)}, u32[]{:S(2)}, u32[]{:S(2)}) collective-permute-start(f32[1,128,128]{2,0,1:T(1,128)S(1)} %get-tuple-element.31), channel_id=1, source_target_pairs={{0,8},{8,16},{16,24},{24,0},{1,9},{9,17},{17,25},{25,1},{2,10},{10... | collective-permute-start | bytes 196616 | tf_op jit(solution)/shard_map/ppermute | solution.py:20
  161.2 8.7 %collective-permute-start.13 = (f32[1,128,128]{2,0,1:T(1,128)S(1)}, f32[1,128,128]{2,0,1:T(1,128)S(1)}, u32[]{:S(2)}, u32[]{:S(2)}) collective-permute-start(f32[1,128,128]{2,0,1:T(1,128)S(1)} %get-tuple-element.30), channel_id=1, source_target_pairs={{8,0},{16,8},{24,16},{0,24},{9,1},{17,9},{25,17},{1,25},{10,2},{18... | collective-permute-start | bytes 196616 | tf_op jit(solution)/shard_map/ppermute | solution.py:22
  165.1 4.8 %collective-permute-start.14 = (f32[32,1,128]{2,0,1:T(8,128)S(1)}, f32[32,1,128]{2,0,1:T(8,128)S(1)}, u32[]{:S(2)}, u32[]{:S(2)}) collective-permute-start(f32[32,1,128]{2,0,1:T(8,128)S(1)} %get-tuple-element.27), channel_id=1, source_target_pairs={{0,2},{2,4},{4,6},{6,0},{1,3},{3,5},{5,7},{7,1},{8,10},{10,12},{12... | collective-permute-start | bytes 49160 | tf_op jit(solution)/shard_map/ppermute | solution.py:20
  165.1 4.8 %collective-permute-start.15 = (f32[32,1,128]{2,0,1:T(8,128)S(1)}, f32[32,1,128]{2,0,1:T(8,128)S(1)}, u32[]{:S(2)}, u32[]{:S(2)}) collective-permute-start(f32[32,1,128]{2,0,1:T(8,128)S(1)} %get-tuple-element.26), channel_id=1, source_target_pairs={{2,0},{4,2},{6,4},{0,6},{3,1},{5,3},{7,5},{1,7},{10,8},{12,10},{14... | collective-permute-start | bytes 49160 | tf_op jit(solution)/shard_map/ppermute | solution.py:22
  192.6 8.6 %collective-permute-start.22 = (f32[32,128,1]{1,0,2:T(8,128)S(1)}, f32[32,128,1]{1,0,2:T(8,128)S(1)}, u32[]{:S(2)}, u32[]{:S(2)}) collective-permute-start(f32[32,128,1]{1,0,2:T(8,128)S(1)} %copy.109), channel_id=1, source_target_pairs={{0,1},{1,0},{2,3},{3,2},{4,5},{5,4},{6,7},{7,6},{8,9},{9,8},{10,11... | collective-permute-start | bytes 49160 | tf_op jit(solution)/shard_map/ppermute | solution.py:20
  196.8 9.2 %collective-permute-start.23 = (f32[32,128,1]{1,0,2:T(8,128)S(1)}, f32[32,128,1]{1,0,2:T(8,128)S(1)}, u32[]{:S(2)}, u32[]{:S(2)}) collective-permute-start(f32[32,128,1]{1,0,2:T(8,128)S(1)} %copy.111), channel_id=1, source_target_pairs={{1,0},{0,1},{3,2},{2,3},{5,4},{4,5},{7,6},{6,7},{9,8},{8,9},{11,10... | collective-permute-start | bytes 49160 | tf_op jit(solution)/shard_map/ppermute | solution.py:22
  197.4 8.7 %collective-permute-start.18 = (f32[1,128,128]{2,0,1:T(1,128)S(1)}, f32[1,128,128]{2,0,1:T(1,128)S(1)}, u32[]{:S(2)}, u32[]{:S(2)}) collective-permute-start(f32[1,128,128]{2,0,1:T(1,128)S(1)} %get-tuple-element.19), channel_id=1, source_target_pairs={{0,8},{8,16},{16,24},{24,0},{1,9},{9,17},{17,25},{25,1},{2,10},{10... | collective-permute-start | bytes 196616 | tf_op jit(solution)/shard_map/ppermute | solution.py:20
  197.4 8.7 %collective-permute-start.19 = (f32[1,128,128]{2,0,1:T(1,128)S(1)}, f32[1,128,128]{2,0,1:T(1,128)S(1)}, u32[]{:S(2)}, u32[]{:S(2)}) collective-permute-start(f32[1,128,128]{2,0,1:T(1,128)S(1)} %get-tuple-element.18), channel_id=1, source_target_pairs={{8,0},{16,8},{24,16},{0,24},{9,1},{17,9},{25,17},{1,25},{10,2},{18... | collective-permute-start | bytes 196616 | tf_op jit(solution)/shard_map/ppermute | solution.py:22
  201.2 4.9 %collective-permute-start.20 = (f32[32,1,128]{2,0,1:T(8,128)S(1)}, f32[32,1,128]{2,0,1:T(8,128)S(1)}, u32[]{:S(2)}, u32[]{:S(2)}) collective-permute-start(f32[32,1,128]{2,0,1:T(8,128)S(1)} %get-tuple-element.15), channel_id=1, source_target_pairs={{0,2},{2,4},{4,6},{6,0},{1,3},{3,5},{5,7},{7,1},{8,10},{10,12},{12... | collective-permute-start | bytes 49160 | tf_op jit(solution)/shard_map/ppermute | solution.py:20
  201.2 4.9 %collective-permute-start.21 = (f32[32,1,128]{2,0,1:T(8,128)S(1)}, f32[32,1,128]{2,0,1:T(8,128)S(1)}, u32[]{:S(2)}, u32[]{:S(2)}) collective-permute-start(f32[32,1,128]{2,0,1:T(8,128)S(1)} %get-tuple-element.14), channel_id=1, source_target_pairs={{2,0},{4,2},{6,4},{0,6},{3,1},{5,3},{7,5},{1,7},{10,8},{12,10},{14... | collective-permute-start | bytes 49160 | tf_op jit(solution)/shard_map/ppermute | solution.py:22
where the time goes:
time: 256 us; the launch traced here: 252 us
  local copies, waits for them, and re-layouts  120 us (47%)
  other arithmetic  66.8 us (26%)
  starting transfers between devices  43.3 us (17%)
  matrix products  18 us (7%)
  between operations  2.62 us (1%)
    div x4, other arithmetic, face_sweep(): return (neighbours + source) / (6.0 + diag_shift)  46.8 us
    slice x12, local copies, waits for them, and re-layouts, face_sweep(): edge_z = jnp.stack([field[:, :, 0], field[:, :, -1]], axis=2)  34.3 us
    gather x1, local copies, waits for them, and re-layouts, on_device(): fetched = row_table[iface_cells // lane_width]  27.9 us
    unnamed x39, local copies, waits for them, and re-layouts  22.5 us
    ppermute x12, starting transfers between devices, extended(): lax.ppermute(head, axis, [((i + 1) % count, i) for i in range(count)])  21.8 us
    dot_general x1, matrix products, on_device(): jnp.dot(selector, incoming.reshape(devices * CAP, 4 * tile_width), precis...  17.6 us
    reduce_sum x1, other arithmetic, on_device(): jnp.sum(jnp.exp(-GAUSS_RATE * distance) * picked[:, :, 0, :], axis=(1, 2))  13.4 us
    ppermute x12, starting transfers between devices, extended(): lax.ppermute(tail, axis, [(i, (i + 1) % count) for i in range(count)])  11.2 us
  transfers between devices with their start and end apart: 26, of which 1 were waited for; matrix products, arithmetic and copies ran while one was open for 66% of the time, Pallas kernels for 0%

commit v1 on v0

v1 whole, which is shorter than its diff:
```python
import functools

import jax
import jax.numpy as jnp
from jax import lax
from jax.experimental import pallas as pl
from jax.experimental.pallas import tpu as pltpu
from jax.sharding import PartitionSpec as P

ITERS = 4
CAP = 4
LANES = 128
SUBLANES = 8
GAUSS_RATE = 0.5
AXES = ("fx", "fy", "fz")
F32 = jnp.float32


def vmem():
    return pl.BlockSpec(memory_space=pltpu.VMEM)


def smem():
    return pl.BlockSpec(memory_space=pltpu.SMEM)


def params(mib):
    return pltpu.CompilerParams(vmem_limit_bytes=mib * 1024 * 1024)


def shape_of(*dims):
    return jax.ShapeDtypeStruct(dims, F32)


def z_pack_dims(cx, cy):
    per = cy // SUBLANES
    planes = LANES // per
    return per, planes, cx // planes


def pack_z(plane, x, zf_ref, per, planes):
    cy = plane.shape[0]
    lane = lax.broadcasted_iota(jnp.int32, (cy, LANES), 1)
    row = lax.broadcasted_iota(jnp.int32, (cy, LANES), 0)
    mine = lane == row // SUBLANES
    shift = (x % planes) * per
    for side, col in ((0, 0), (1, LANES - 1)):
        spread = jnp.broadcast_to(plane[:, col : col + 1], (cy, LANES))
        kept = jnp.where(mine, spread, 0.0).reshape(per, SUBLANES, LANES)
        moved = pltpu.roll(jnp.sum(kept, axis=0), shift, 1)
        zf_ref[side, x // planes] = zf_ref[side, x // planes] + moved


def unpack_z(packed, x, per, planes):
    back = (LANES - (x % planes) * per) % LANES
    rolled = pltpu.roll(packed, back, 1)
    parts = [jnp.broadcast_to(rolled[:, j : j + 1], (SUBLANES, LANES)) for j in range(per)]
    return jnp.concatenate(parts, axis=0)


def emit_y(plane, x, ylo_ref, yhi_ref):
    ylo_ref[pl.ds(x, 1), :] = plane[0:1]
    yhi_ref[pl.ds(x, 1), :] = plane[plane.shape[0] - 1 :]


def faces_kernel(p_ref, ylo_ref, yhi_ref, zf_ref):
    cx, cy, _ = p_ref.shape
    per, planes, _ = z_pack_dims(cx, cy)
    zf_ref[...] = jnp.zeros(zf_ref.shape, F32)

    def step(x, carry):
        plane = p_ref[x]
        emit_y(plane, x, ylo_ref, yhi_ref)
        pack_z(plane, x, zf_ref, per, planes)
        return carry

    lax.fori_loop(0, cx, step, 0)


def sweep_kernel(first, last, swap, *refs):
    p_ref, src_ref, inv_in_ref, xlo_ref, xhi_ref, ylo_ref, yhi_ref, zr_ref = refs[:8]
    outs = refs[8:]
    out_ref = outs[0]
    outs = outs[1:]
    if first:
        inv_out_ref = outs[0]
        outs = outs[1:]
    cx, cy, cz = p_ref.shape
    per, planes, _ = z_pack_dims(cx, cy)
    zlo_at, zhi_at = (1, 0) if swap else (0, 1)
    if not last:
        xlo_out, xhi_out, ylo_out, yhi_out, zf_ref = outs
        zf_ref[...] = jnp.zeros(zf_ref.shape, F32)
    lane = lax.broadcasted_iota(jnp.int32, (cy, cz), 1)

    def one(x, below, above):
        here = p_ref[x]
        total = below + above
        total = total + jnp.concatenate([ylo_ref[pl.ds(x, 1), :], here[: cy - 1]], axis=0)
        total = total + jnp.concatenate([here[1:], yhi_ref[pl.ds(x, 1), :]], axis=0)
        zlo = unpack_z(zr_ref[zlo_at, x // planes], x, per, planes)
        zhi = unpack_z(zr_ref[zhi_at, x // planes], x, per, planes)
        total = total + jnp.where(lane == 0, zlo, pltpu.roll(here, 1, 1))
        total = total + jnp.where(lane == cz - 1, zhi, pltpu.roll(here, cz - 1, 1))
        if first:
            inv = 1.0 / (6.0 + inv_in_ref[x])
            inv_out_ref[x] = inv
        else:
            inv = inv_in_ref[x]
        result = (total + src_ref[x]) * inv
        out_ref[x] = result
        if not last:
            emit_y(result, x, ylo_out, yhi_out)
            pack_z(result, x, zf_ref, per, planes)
        return result

    result = one(0, xlo_ref[0], p_ref[1])
    if not last:
        xlo_out[0] = result

    def step(x, carry):
        one(x, p_ref[x - 1], p_ref[x + 1])
        return carry

    lax.fori_loop(1, cx - 1, step, 0)
    result = one(cx - 1, p_ref[cx - 2], xhi_ref[0])
    if not last:
        xhi_out[0] = result


def gather_kernel(row_ref, target_ref, p_ref, lane_ref, coef_ref, xyz_ref, out_ref):
    tiles, width = coef_ref.shape
    out_ref[...] = jnp.zeros(out_ref.shape, F32)
    sub = lax.broadcasted_iota(jnp.int32, (SUBLANES, LANES), 0)
    lane = lax.broadcasted_iota(jnp.int32, (SUBLANES, LANES), 1)

    def tile_step(t, carry):
        pick = jnp.broadcast_to(lane_ref[pl.ds(t, 1), :], (SUBLANES, LANES))
        total = jnp.zeros((SUBLANES, LANES), F32)
        for group in range(width // SUBLANES):
            rows = None
            for s in range(SUBLANES):
                at = row_ref[t * width + group * SUBLANES + s]
                row = jnp.broadcast_to(p_ref[pl.ds(at, 1), :], (SUBLANES, LANES))
                rows = row if rows is None else jnp.where(sub == s, row, rows)
            picked = jnp.take_along_axis(rows, pick, axis=1, mode="promise_in_bounds")
            total = jnp.where(lane == sub + group * SUBLANES, picked, total)
        values = jnp.sum(total, axis=0, keepdims=True) * coef_ref[pl.ds(t, 1), :]
        slot = target_ref[t]
        out_ref[slot, 0:1, :] = values
        for c in range(3):
            out_ref[slot, c + 1 : c + 2, :] = xyz_ref[c, pl.ds(t, 1), :]
        return carry

    lax.fori_loop(0, tiles, tile_step, 0)


def lane_gather(row, chunks, low, high):
    got = None
    for at in range(chunks):
        part = jnp.broadcast_to(row[:, at * LANES : (at + 1) * LANES], (SUBLANES, LANES))
        part = jnp.take_along_axis(part, low, axis=1, mode="promise_in_bounds")
        got = part if got is None else jnp.where(high == at, part, got)
    return got


def node_kernel(inc_ref, wanted_ref, slot_ref, node_ref, out_ref, table_ref):
    slots = inc_ref.shape[0]
    width = inc_ref.shape[2]
    neigh, rows, _ = wanted_ref.shape
    chunks = slots // LANES
    scale = GAUSS_RATE ** 0.5
    for c in range(4):
        part = inc_ref[:, c, :]
        if c > 0:
            part = part * scale
        table_ref[c] = part.T
    slot_row = slot_ref[...]

    def pair(step, carry):
        k = step % neigh
        block = step // neigh
        at = pl.ds(pl.multiple_of(block * SUBLANES, SUBLANES), SUBLANES)
        wanted = wanted_ref[k, at, :]
        chosen = lane_gather(slot_row, chunks, wanted % LANES, wanted // LANES)
        low = chosen % LANES
        high = chosen // LANES
        coords = [node_ref[c, at, :] * scale for c in range(3)]
        before = jnp.where(k == 0, 0.0, out_ref[at, :])

        def points(base, total):
            for u in range(16):
                p = base * 16 + u
                got = [
                    lane_gather(table_ref[c, pl.ds(p, 1), :], chunks, low, high) for c in range(4)
                ]
                gaps = [coords[c] - got[c + 1] for c in range(3)]
                dist = gaps[0] * gaps[0] + gaps[1] * gaps[1] + gaps[2] * gaps[2]
                total = total + jnp.exp(-dist) * got[0]
            return total

        out_ref[at, :] = lax.fori_loop(0, width // 16, points, before)
        return carry

    lax.fori_loop(0, neigh * (rows // SUBLANES), pair, 0)


def ring(axis, up):
    count = lax.axis_size(axis)
    if up:
        return [(i, (i + 1) % count) for i in range(count)]
    return [((i + 1) % count, i) for i in range(count)]


def exchange(xlo, xhi, ylo, yhi, zf):
    from_x_lo = lax.ppermute(xhi, "fx", ring("fx", True))
    from_x_hi = lax.ppermute(xlo, "fx", ring("fx", False))
    from_y_lo = lax.ppermute(yhi, "fy", ring("fy", True))
    from_y_hi = lax.ppermute(ylo, "fy", ring("fy", False))
    if lax.axis_size("fz") == 2:
        z = lax.ppermute(zf, "fz", ring("fz", True))
    else:
        z = jnp.stack(
            [
                lax.ppermute(zf[1], "fz", ring("fz", True)),
                lax.ppermute(zf[0], "fz", ring("fz", False)),
            ]
        )
    return from_x_lo, from_x_hi, from_y_lo, from_y_hi, z


def on_device(
    pressure, source, diag_shift, iface_cells, iface_coef, iface_xyz, node_xyz, owners, node_lists
):
    devices = lax.axis_size(AXES)
    cx, cy, cz = pressure.shape
    tiles_dev = owners.shape[0]
    width = iface_coef.shape[0] // tiles_dev
    node_count, neigh = node_lists.shape
    slots = devices * CAP
    per, planes, packs = z_pack_dims(cx, cy)
    y_shape = shape_of(cx, cz)
    z_shape = shape_of(2, packs, SUBLANES, LANES)
    x_shape = shape_of(1, cy, cz)
    block = shape_of(cx, cy, cz)

    owned_by = (owners[:, None] == jnp.arange(devices, dtype=jnp.int32)[None, :]).astype(jnp.int32)
    order = lax.broadcasted_iota(jnp.int32, (tiles_dev, tiles_dev), 0)
    other = lax.broadcasted_iota(jnp.int32, (tiles_dev, tiles_dev), 1)
    same = (owners[:, None] == owners[None, :]) & (other < order)
    target = owners * CAP + jnp.sum(same.astype(jnp.int32), axis=1)
    counts = jnp.sum(owned_by, axis=0)
    filled = (jnp.arange(CAP, dtype=jnp.int32)[None, :] < counts[:, None]).astype(F32)
    arrived = lax.all_to_all(filled, AXES, split_axis=0, concat_axis=0, tiled=True)
    arrived = arrived.reshape(slots).astype(jnp.int32)
    lower = lax.broadcasted_iota(jnp.int32, (slots, slots), 1) <= lax.broadcasted_iota(
        jnp.int32, (slots, slots), 0
    )
    prefix = jnp.sum(jnp.where(lower, arrived[None, :], 0), axis=1)
    owned_count = jnp.sum(arrived)
    entry = jnp.arange(slots, dtype=jnp.int32)
    hit = (prefix[None, :] == entry[:, None] + 1) & (arrived[None, :] > 0)
    slot_of = jnp.sum(jnp.where(hit, entry[None, :], 0), axis=1).reshape(1, slots)
    wanted = (node_lists.T % owned_count).reshape(neigh, node_count // LANES, LANES)

    ylo, yhi, zf = pl.pallas_call(
        faces_kernel,
        out_shape=(y_shape, y_shape, z_shape),
        in_specs=[vmem()],
        out_specs=(vmem(),) * 3,
        compiler_params=params(8),
        name="faces",
    )(pressure)
    halos = exchange(pressure[:1], pressure[cx - 1 :], ylo, yhi, zf)

    outgoing = pl.pallas_call(
        gather_kernel,
        out_shape=shape_of(slots, 4, width),
        in_specs=[smem(), smem(), vmem(), vmem(), vmem(), vmem()],
        out_specs=vmem(),
        compiler_params=params(12),
        name="cells",
    )(
        iface_cells // cz,
        target,
        pressure.reshape(cx * cy, cz),
        (iface_cells % cz).reshape(tiles_dev, width),
        iface_coef.reshape(tiles_dev, width),
        iface_xyz.reshape(3, tiles_dev, width),
    )
    incoming = lax.all_to_all(outgoing, AXES, split_axis=0, concat_axis=0, tiled=True)

    swap = lax.axis_size("fz") == 2
    current, inverse = pressure, diag_shift
    for index in range(ITERS):
        first, last = index == 0, index == ITERS - 1
        shapes = [block]
        if first:
            shapes.append(block)
        if not last:
            shapes += [x_shape, x_shape, y_shape, y_shape, z_shape]
        results = pl.pallas_call(
            functools.partial(sweep_kernel, first, last, swap),
            out_shape=tuple(shapes),
            in_specs=[vmem()] * 8,
            out_specs=tuple(vmem() for _ in shapes),
            compiler_params=params(16),
            name="sweep",
        )(current, source, inverse, *halos)
        current = results[0]
        if first:
            inverse = results[1]
        if not last:
            halos = exchange(*results[-5:])

    loads = pl.pallas_call(
        node_kernel,
        out_shape=shape_of(node_count // LANES, LANES),
        in_specs=[vmem()] * 4,
        out_specs=vmem(),
        scratch_shapes=[pltpu.VMEM((4, width, slots), F32)],
        compiler_params=params(12),
        name="nodes",
    )(incoming, wanted, slot_of, node_xyz.reshape(3, node_count // LANES, LANES))
    return current, loads.reshape(node_count)


def solution(mesh):
    placed = (
        P("fx", "fy", "fz"),
        P("fx", "fy", "fz"),
        P("fx", "fy", "fz"),
        P(AXES),
        P(AXES),
        P(None, AXES),
        P(None, AXES),
        P(AXES),
        P(AXES, None),
    )
    return jax.shard_map(
        on_device,
        mesh=mesh,
        in_specs=placed,
        out_specs=(P("fx", "fy", "fz"), P(AXES)),
        check_vma=False,
    )
```

time: 256 us -> 137 us (0.54); the launches traced: 252 us -> 135 us
  local copies, waits for them, and re-layouts: 120 us -> 7.39 us
  Pallas kernels: 0 us -> 81 us
  other arithmetic: 66.8 us -> 2.66 us
  matrix products: 18 us -> 0 us
  starting transfers between devices: 43.3 us -> 37.7 us
  waiting for transfers between devices: 0.99 us -> 4.38 us
    pallas_call x0 -> x7, Pallas kernels: none -> 81 us  [the longest x4 41.4 us: on_device(): pl.pallas_call(functools.partial(sweep_kernel, first, last, swap), out_sh...]
    slice x34 -> x1, local copies, waits for them, and re-layouts: 67.1 us -> 0.88 us  [on_device(): halos = exchange(pressure[:1], pressure[cx - 1:], ylo, yhi, zf)]
    div x4 -> x0, other arithmetic: 46.8 us -> none  [face_sweep(): return (neighbours + source) / (6.0 + diag_shift)]
    gather x1 -> x0, local copies, waits for them, and re-layouts: 27.9 us -> none  [on_device(): fetched = row_table[iface_cells // lane_width]]
    reduce_sum x4, other arithmetic: 18.5 us -> 0.56 us  [the longest x1 0.17 us: on_device(): target = owners * CAP + jnp.sum(same.astype(jnp.int32), axis=1)]
    dot_general x2 -> x0, matrix products: 18 us -> none  [the longest x1 17.6 us: on_device(): jnp.dot(selector, incoming.reshape(devices * CAP, 4 * tile_width), precis...]
    unnamed x39 -> x25, local copies, waits for them, and re-layouts: 22.5 us -> 6.41 us
    ppermute x24 -> x20, starting transfers between devices: 33 us -> 28.8 us  [the longest x4 11.9 us: exchange(): from_x_hi = lax.ppermute(xlo, 'fx', ring('fx', False))]
  transfers between devices with their start and end apart: 26 -> 22, of which waited for: 1 -> 4; matrix products, arithmetic and copies ran while one was open for 66% -> 3% of each run, Pallas kernels for 0% -> 40%
where the time goes in v1:
time: 137 us; the launch traced here: 135 us
  Pallas kernels  81 us (59%)
  starting transfers between devices  37.7 us (28%)
  local copies, waits for them, and re-layouts  7.39 us (5%)
  waiting for transfers between devices  4.38 us (3%)
  other arithmetic  2.66 us (2%)
  between operations  2.18 us (2%)
    pallas_call x4, Pallas kernels, on_device(): pl.pallas_call(functools.partial(sweep_kernel, first, last, swap), out_sh...  41.4 us
    pallas_call x1, Pallas kernels, on_device(): pl.pallas_call(node_kernel, out_shape=shape_of(node_count // LANES, LANES...  20.8 us
    pallas_call x1, Pallas kernels, on_device(): pl.pallas_call(gather_kernel, out_shape=shape_of(slots, 4, width), in_spe...  13.3 us
    ppermute x4, starting transfers between devices, exchange(): from_x_hi = lax.ppermute(xlo, 'fx', ring('fx', False))  11.9 us
    ppermute x4, starting transfers between devices, exchange(): z = lax.ppermute(zf, 'fz', ring('fz', True))  6.48 us
    unnamed x25, local copies, waits for them, and re-layouts  6.41 us
    all_to_all x1, starting transfers between devices, on_device(): lax.all_to_all(outgoing, AXES, split_axis=0, concat_axis=0, tiled=True)  5.83 us
    ppermute x4, starting transfers between devices, exchange(): from_y_hi = lax.ppermute(ylo, 'fy', ring('fy', False))  5.71 us
  transfers between devices with their start and end apart: 22, of which 4 were waited for; matrix products, arithmetic and copies ran while one was open for 3% of the time, Pallas kernels for 40%

profile of v1, /device:TPU:0, one launch (start us, length us, event | category | flops | bytes accessed | tf_op | source)
XLA Modules:
  0.0 135.3 jit_solution(16858785450007788060)
XLA Ops:
  0.6 0.0 copy-start.1
  0.6 1.6 %copy-done.1 = f32[32,128,128]{2,1,0:T(8,128)S(1)} copy-done((f32[32,128,128]{2,1,0:T(8,128)S(1)}, f32[32,128,128]{2,1,0:T(8,128)}, u32[]{:S(2)}) %copy-start.1) | copy-done | bytes 2097176
  2.3 5.5 %faces.1 = (f32[32,128]{1,0:T(8,128)S(1)}, f32[32,128]{1,0:T(8,128)S(1)}, f32[2,4,8,128]{3,2,1,0:T(8,128)S(1)}) custom-call(f32[32,128,128]{2,1,0:T(8,128)S(1)} %copy-done.1), custom_call_target="tpu_custom_call" | custom-call | tf_op jit(solution)/shard_map/faces/pallas_call | solution.py:266
  7.7 3.0 %collective-permute-start.4 = (f32[2,4,8,128]{3,2,1,0:T(8,128)S(1)}, f32[2,4,8,128]{3,2,1,0:T(8,128)S(1)}, u32[]{:S(2)}, u32[]{:S(2)}) collective-permute-start(f32[2,4,8,128]{3,2,1,0:T(8,128)S(1)} %get-tuple-element.26), channel_id=1, source_target_pairs={{0,1},{1,0},{2,3},{3,2},{4,5},{5,4},{6,7},{7,6},{8,9},{9,8},{10,11... | collective-permute-start | bytes 98312 | tf_op jit(solution)/shard_map/ppermute | solution.py:221
  10.7 0.0 collective-permute-start.2
  10.7 1.7 %collective-permute-start.3 = (f32[32,128]{1,0:T(8,128)S(1)}, f32[32,128]{1,0:T(8,128)S(1)}, u32[]{:S(2)}, u32[]{:S(2)}) collective-permute-start(f32[32,128]{1,0:T(8,128)S(1)} %get-tuple-element.25), channel_id=1, source_target_pairs={{2,0},{4,2},{6,4},{0,6},{3,1},{5,3},{7,5},{1,7},{10,8},{12,10},{14... | collective-permute-start | bytes 49160 | tf_op jit(solution)/shard_map/ppermute | solution.py:219
  12.5 0.9 fusion.7
  13.4 1.6 %collective-permute-start = (f32[1,128,128]{2,1,0:T(8,128)S(1)}, f32[1,128,128]{2,1,0:T(8,128)S(1)}, u32[]{:S(2)}, u32[]{:S(2)}) collective-permute-start(f32[1,128,128]{2,1,0:T(8,128)S(1)} %get-tuple-element.49), channel_id=1, source_target_pairs={{0,8},{8,16},{16,24},{24,0},{1,9},{9,17},{17,25},{25,1},{2,10},{10... | collective-permute-start | bytes 196616 | tf_op jit(solution)/shard_map/ppermute | solution.py:216
  15.0 2.2 %collective-permute-start.1 = (f32[1,128,128]{2,1,0:T(8,128)S(1)}, f32[1,128,128]{2,1,0:T(8,128)S(1)}, u32[]{:S(2)}, u32[]{:S(2)}) collective-permute-start(f32[1,128,128]{2,1,0:T(8,128)S(1)} %get-tuple-element.48), channel_id=1, source_target_pairs={{8,0},{16,8},{24,16},{0,24},{9,1},{17,9},{25,17},{1,25},{10,2},{18... | collective-permute-start | bytes 196616 | tf_op jit(solution)/shard_map/ppermute | solution.py:217
  17.3 0.1 convert_reduce_fusion.3
  17.4 0.7 compare_convert_fusion
  18.1 3.1 %all-to-all-start.1 = ((f32[32,1,4]{2,1,0:T(1,128)}), f32[32,1,4]{2,1,0:T(1,128)S(1)}, u32[]{:S(2)}, u32[]{:S(2)}) async-start(f32[32,1,4]{2,1,0:T(1,128)} %compare_convert_fusion), calls=%async_computation.1 | async-start | bytes 32768 | tf_op jit(solution)/shard_map/all_to_all | solution.py:254
  21.2 0.2 convert_reduce_fusion
  21.5 0.0 copy-start.2
  21.5 1.6 %copy-done.2 = f32[32,128,128]{2,1,0:T(8,128)S(1)} copy-done((f32[32,128,128]{2,1,0:T(8,128)S(1)}, f32[32,128,128]{2,1,0:T(8,128)}, u32[]{:S(2)}) %copy-start.2) | copy-done | bytes 2097176
  23.1 13.3 %cells.1 = f32[128,4,128]{2,1,0:T(4,128)} custom-call(s32[8192]{0:T(1024)S(1)} %get-tuple-element.51.row_ref, s32[64]{0:T(128)S(1)} %multiply_add_fusion.target_ref, f32[4096,128]{1,0:T(8,128)S(1)} %bitcast.31, s32[64,128]{1,0:T(8,128)S(1)} %get-tuple-element.50.lane_ref, f32[64,128]{1,0:T(8,128)S(1)} %bitcast.35, f32[3,64,128]{2,1,0:T(8,128)S(1)} %bitcast.32), custom_call_target="tpu_custom_call" | custom-call | tf_op jit(solution)/shard_map/cells/pallas_call | solution.py:276
  36.4 0.0 all-to-all-done.1
  36.4 5.8 %all-to-all-start = ((f32[128,4,128]{2,1,0:T(4,128)}), f32[128,4,128]{2,1,0:T(4,128)S(1)}, u32[]{:S(2)}, u32[]{:S(2)}) async-start(f32[128,4,128]{2,1,0:T(4,128)} %cells.1), calls=%async_computation | async-start | bytes 524288 | tf_op jit(solution)/shard_map/all_to_all | solution.py:291
  42.2 0.7 convert_reduce_fusion.1
  44.2 0.7 fusion
  44.9 0.1 convert_element_type.35
  45.0 0.0 collective-permute-done.2.refs_5_
  45.0 0.0 collective-permute-done.3.refs_6_
  45.0 0.0 collective-permute-done.4.refs_7_
  45.0 0.0 collective-permute-done.refs_3_
  45.0 0.0 collective-permute-done.1.refs_4_
  45.0 0.0 copy-start.3
  45.0 1.6 %copy-done.3 = f32[32,128,128]{2,1,0:T(8,128)S(1)} copy-done((f32[32,128,128]{2,1,0:T(8,128)S(1)}, f32[32,128,128]{2,1,0:T(8,128)}, u32[]{:S(2)}) %copy-start.3) | copy-done | bytes 2097176
  46.6 1.6 %copy-done.4 = f32[32,128,128]{2,1,0:T(8,128)S(1)} copy-done((f32[32,128,128]{2,1,0:T(8,128)S(1)}, f32[32,128,128]{2,1,0:T(8,128)}, u32[]{:S(2)}) %copy-start.4) | copy-done | bytes 2097176
  48.2 11.1 %sweep.4 = (f32[32,128,128]{2,1,0:T(8,128)S(1)}, f32[32,128,128]{2,1,0:T(8,128)S(1)}, f32[1,128,128]{2,1,0:T(8,128)S(1)}, f32[1,128,128]{2,1,0:T(8,128)S(1)}, f3...) custom-call(f32[32,128,128]{2,1,0:T(8,128)S(1)} %copy-done.3, ...), custom_call_target="tpu_custom_call" | custom-call | tf_op jit(solution)/shard_map/sweep/pallas_call | solution.py:302
  59.3 1.8 %collective-permute-start.5 = (f32[1,128,128]{2,1,0:T(8,128)S(1)}, f32[1,128,128]{2,1,0:T(8,128)S(1)}, u32[]{:S(2)}, u32[]{:S(2)}) collective-permute-start(f32[1,128,128]{2,1,0:T(8,128)S(1)} %get-tuple-element.29), channel_id=1, source_target_pairs={{0,8},{8,16},{16,24},{24,0},{1,9},{9,17},{17,25},{25,1},{2,10},{10... | collective-permute-start | bytes 196616 | tf_op jit(solution)/shard_map/ppermute | solution.py:216
  61.1 2.1 %collective-permute-start.6 = (f32[1,128,128]{2,1,0:T(8,128)S(1)}, f32[1,128,128]{2,1,0:T(8,128)S(1)}, u32[]{:S(2)}, u32[]{:S(2)}) collective-permute-start(f32[1,128,128]{2,1,0:T(8,128)S(1)} %get-tuple-element.30), channel_id=1, source_target_pairs={{8,0},{16,8},{24,16},{0,24},{9,1},{17,9},{25,17},{1,25},{10,2},{18... | collective-permute-start | bytes 196616 | tf_op jit(solution)/shard_map/ppermute | solution.py:217
  63.2 1.8 %collective-permute-start.9 = (f32[2,4,8,128]{3,2,1,0:T(8,128)S(1)}, f32[2,4,8,128]{3,2,1,0:T(8,128)S(1)}, u32[]{:S(2)}, u32[]{:S(2)}) collective-permute-start(f32[2,4,8,128]{3,2,1,0:T(8,128)S(1)} %get-tuple-element.33), channel_id=1, source_target_pairs={{0,1},{1,0},{2,3},{3,2},{4,5},{5,4},{6,7},{7,6},{8,9},{9,8},{10,11... | collective-permute-start | bytes 98312 | tf_op jit(solution)/shard_map/ppermute | solution.py:221
  64.9 0.0 collective-permute-start.7
  64.9 1.7 %collective-permute-start.8 = (f32[32,128]{1,0:T(8,128)S(1)}, f32[32,128]{1,0:T(8,128)S(1)}, u32[]{:S(2)}, u32[]{:S(2)}) collective-permute-start(f32[32,128]{1,0:T(8,128)S(1)} %get-tuple-element.32), channel_id=1, source_target_pairs={{2,0},{4,2},{6,4},{0,6},{3,1},{5,3},{7,5},{1,7},{10,8},{12,10},{14... | collective-permute-start | bytes 49160 | tf_op jit(solution)/shard_map/ppermute | solution.py:219
  66.7 1.4 %collective-permute-done.7.refs_5_ = f32[32,128]{1,0:T(8,128)S(1)} collective-permute-done((f32[32,128]{1,0:T(8,128)S(1)}, f32[32,128]{1,0:T(8,128)S(1)}, u32[]{:S(2)}, u32[]{:S(2)}) %collective-permute-start.7) | collective-permute-done | bytes 16416 | tf_op jit(solution)/shard_map/ppermute | solution.py:218
  68.1 0.0 collective-permute-done.8.refs_6_
  68.1 0.0 collective-permute-done.9.refs_7_
  68.1 0.0 collective-permute-done.5.refs_3_
  68.1 0.0 collective-permute-done.6.refs_4_
  68.1 11.1 %sweep.5 = (f32[32,128,128]{2,1,0:T(8,128)S(1)}, f32[1,128,128]{2,1,0:T(8,128)S(1)}, f32[1,128,128]{2,1,0:T(8,128)S(1)}, f32[32,128]{1,0:T(8,128)S(1)}, f32[32,1...) custom-call(f32[32,128,128]{2,1,0:T(8,128)S(1)} %get-tuple-element.27.refs_0_, f32[32,128,128]{2,1,0:T(8,128)S(1)} %copy-done, ...), custom_call_target="tpu_custom_call" | custom-call | tf_op jit(solution)/shard_map/sweep/pallas_call | solution.py:302
  79.3 0.0 collective-permute-start.10
  79.3 3.8 %collective-permute-start.11 = (f32[1,128,128]{2,1,0:T(8,128)S(1)}, f32[1,128,128]{2,1,0:T(8,128)S(1)}, u32[]{:S(2)}, u32[]{:S(2)}) collective-permute-start(f32[1,128,128]{2,1,0:T(8,128)S(1)} %get-tuple-element.36), channel_id=1, source_target_pairs={{8,0},{16,8},{24,16},{0,24},{9,1},{17,9},{25,17},{1,25},{10,2},{18... | collective-permute-start | bytes 196616 | tf_op jit(solution)/shard_map/ppermute | solution.py:217
  83.1 0.7 collective-permute-start.14
  83.8 0.6 collective-permute-start.12
  84.4 1.2 collective-permute-start.13
  85.6 0.1 select_reduce_fusion.1
  85.7 1.3 collective-permute-done.12.refs_5_
  87.0 0.0 collective-permute-done.13.refs_6_
  87.0 0.3 collective-permute-done.14.refs_7_
  87.4 0.0 collective-permute-done.11.refs_4_
  87.4 11.1 %sweep.6 = (f32[32,128,128]{2,1,0:T(8,128)S(1)}, f32[1,128,128]{2,1,0:T(8,128)S(1)}, f32[1,128,128]{2,1,0:T(8,128)S(1)}, f32[32,128]{1,0:T(8,128)S(1)}, f32[32,1...) custom-call(f32[32,128,128]{2,1,0:T(8,128)S(1)} %get-tuple-element.34.refs_0_, f32[32,128,128]{2,1,0:T(8,128)S(1)} %copy-done, ...), custom_call_target="tpu_custom_call" | custom-call | tf_op jit(solution)/shard_map/sweep/pallas_call | solution.py:302
  98.5 0.0 collective-permute-start.15
  98.5 3.8 %collective-permute-start.16 = (f32[1,128,128]{2,1,0:T(8,128)S(1)}, f32[1,128,128]{2,1,0:T(8,128)S(1)}, u32[]{:S(2)}, u32[]{:S(2)}) collective-permute-start(f32[1,128,128]{2,1,0:T(8,128)S(1)} %get-tuple-element.42), channel_id=1, source_target_pairs={{8,0},{16,8},{24,16},{0,24},{9,1},{17,9},{25,17},{1,25},{10,2},{18... | collective-permute-start | bytes 196616 | tf_op jit(solution)/shard_map/ppermute | solution.py:217
  102.3 1.0 collective-permute-start.19
  103.3 0.7 collective-permute-start.17
  104.0 1.0 collective-permute-start.18
  105.1 0.2 select_reduce_fusion
  105.3 1.2 collective-permute-done.17.refs_5_
  106.5 0.0 collective-permute-done.18.refs_6_
  106.5 0.0 collective-permute-done.19.refs_7_
  106.5 8.0 %sweep.7 = f32[32,128,128]{2,1,0:T(8,128)} custom-call(f32[32,128,128]{2,1,0:T(8,128)S(1)} %get-tuple-element.40.refs_0_, f32[32,128,128]{2,1,0:T(8,128)S(1)} %copy-done, f32[32,128,128]{2,1,0:T(8,128)S(1)} %get-tuple-element.28.refs_2_, f32[1,128,128]{2,1,0:T(8,128)S(1)} %collective-permute-done.15.refs_3_, ...), custom_call_target="tpu_custom_call" | custom-call | tf_op jit(solution)/shard_map/sweep/pallas_call | solution.py:302
  114.5 0.0 all-to-all-done.inc_ref
  114.5 20.8 %nodes.1 = f32[16,128]{1,0:T(8,128)} custom-call(f32[128,4,128]{2,1,0:T(4,128)S(1)} %all-to-all-done.inc_ref, s32[8,16,128]{2,1,0:T(8,128)S(1)} %bitcast.33, s32[1,128]{1,0:T(1,128)S(1)} %bitcast.36, f32[3,16,128]{2,1,0:T(8,128)S(1)} %bitcast.34), custom_call_target="tpu_custom_call" | custom-call | tf_op jit(solution)/shard_map/nodes/pallas_call | solution.py:316
  (25 shorter events, 0.1 us)
Async XLA Ops:
  0.6 1.6 %copy-start.1 = (f32[32,128,128]{2,1,0:T(8,128)S(1)}, f32[32,128,128]{2,1,0:T(8,128)}, u32[]{:S(2)}) copy-start(f32[32,128,128]{2,1,0:T(8,128)} %refs_0_.1) | copy-start | bytes 6291460
  2.2 15.0 %copy-start.10 = (s32[64]{0:T(128)S(1)}, s32[64]{0:T(128)}, u32[]{:S(2)}) copy-start(s32[64]{0:T(128)} %param.16) | copy-start | bytes 772
  2.2 19.1 %copy-start.8 = (s32[8192]{0:T(1024)S(1)}, s32[8192]{0:T(1024)}, u32[]{:S(2)}) copy-start(s32[8192]{0:T(1024)} %param.12) | copy-start | bytes 98308
  2.2 19.2 %copy-start.6 = (f32[3,8192]{1,0:T(4,128)S(1)}, f32[3,8192]{1,0:T(4,128)}, u32[]{:S(2)}) copy-start(f32[3,8192]{1,0:T(4,128)} %param.14) | copy-start | bytes 294916
  2.2 19.2 %copy-start.9 = (f32[3,2048]{1,0:T(4,128)S(1)}, f32[3,2048]{1,0:T(4,128)}, u32[]{:S(2)}) copy-start(f32[3,2048]{1,0:T(4,128)} %param.15) | copy-start | bytes 73732
  2.2 19.2 %copy-start.5 = (f32[8192]{0:T(1024)S(1)}, f32[8192]{0:T(1024)}, u32[]{:S(2)}) copy-start(f32[8192]{0:T(1024)} %param.13) | copy-start | bytes 98308
  2.2 41.9 %copy-start.7 = (s32[2048,8]{0,1:T(8,128)S(1)}, s32[2048,8]{0,1:T(8,128)}, u32[]{:S(2)}) copy-start(s32[2048,8]{0,1:T(8,128)} %param.17) | copy-start | bytes 196612
  7.7 37.3 %copy-start = (f32[32,128,128]{2,1,0:T(8,128)S(1)}, f32[32,128,128]{2,1,0:T(8,128)}, u32[]{:S(2)}) copy-start(f32[32,128,128]{2,1,0:T(8,128)} %refs_1_.7) | copy-start | bytes 6291460
  7.7 37.3 %collective-permute-start.4 = (f32[2,4,8,128]{3,2,1,0:T(8,128)S(1)}, f32[2,4,8,128]{3,2,1,0:T(8,128)S(1)}, u32[]{:S(2)}, u32[]{:S(2)}) collective-permute-start(f32[2,4,8,128]{3,2,1,0:T(8,128)S(1)} %get-tuple-element.26), channel_id=1, source_target_pairs={{0,1},{1,0},{2,3},{3,2},{4,5},{5,4},{6,7},{7,6},{8,9},{9,8},{10,11... | collective-permute-start | bytes 98312 | tf_op jit(solution)/shard_map/ppermute | solution.py:221
  10.7 34.2 %collective-permute-start.2 = (f32[32,128]{1,0:T(8,128)S(1)}, f32[32,128]{1,0:T(8,128)S(1)}, u32[]{:S(2)}, u32[]{:S(2)}) collective-permute-start(f32[32,128]{1,0:T(8,128)S(1)} %get-tuple-element.24), channel_id=1, source_target_pairs={{0,2},{2,4},{4,6},{6,0},{1,3},{3,5},{5,7},{7,1},{8,10},{10,12},{12... | collective-permute-start | bytes 49160 | tf_op jit(solution)/shard_map/ppermute | solution.py:218
  10.7 34.2 %collective-permute-start.3 = (f32[32,128]{1,0:T(8,128)S(1)}, f32[32,128]{1,0:T(8,128)S(1)}, u32[]{:S(2)}, u32[]{:S(2)}) collective-permute-start(f32[32,128]{1,0:T(8,128)S(1)} %get-tuple-element.25), channel_id=1, source_target_pairs={{2,0},{4,2},{6,4},{0,6},{3,1},{5,3},{7,5},{1,7},{10,8},{12,10},{14... | collective-permute-start | bytes 49160 | tf_op jit(solution)/shard_map/ppermute | solution.py:219
  13.4 31.6 %collective-permute-start = (f32[1,128,128]{2,1,0:T(8,128)S(1)}, f32[1,128,128]{2,1,0:T(8,128)S(1)}, u32[]{:S(2)}, u32[]{:S(2)}) collective-permute-start(f32[1,128,128]{2,1,0:T(8,128)S(1)} %get-tuple-element.49), channel_id=1, source_target_pairs={{0,8},{8,16},{16,24},{24,0},{1,9},{9,17},{17,25},{25,1},{2,10},{10... | collective-permute-start | bytes 196616 | tf_op jit(solution)/shard_map/ppermute | solution.py:216
  15.0 30.0 %collective-permute-start.1 = (f32[1,128,128]{2,1,0:T(8,128)S(1)}, f32[1,128,128]{2,1,0:T(8,128)S(1)}, u32[]{:S(2)}, u32[]{:S(2)}) collective-permute-start(f32[1,128,128]{2,1,0:T(8,128)S(1)} %get-tuple-element.48), channel_id=1, source_target_pairs={{8,0},{16,8},{24,16},{0,24},{9,1},{17,9},{25,17},{1,25},{10,2},{18... | collective-permute-start | bytes 196616 | tf_op jit(solution)/shard_map/ppermute | solution.py:217
  18.1 18.3 %all-to-all-start.1 = ((f32[32,1,4]{2,1,0:T(1,128)}), f32[32,1,4]{2,1,0:T(1,128)S(1)}, u32[]{:S(2)}, u32[]{:S(2)}) async-start(f32[32,1,4]{2,1,0:T(1,128)} %compare_convert_fusion), calls=%async_computation.1 | async-start | bytes 32768 | tf_op jit(solution)/shard_map/all_to_all | solution.py:254
  21.5 1.6 %copy-start.2 = (f32[32,128,128]{2,1,0:T(8,128)S(1)}, f32[32,128,128]{2,1,0:T(8,128)}, u32[]{:S(2)}) copy-start(f32[32,128,128]{2,1,0:T(8,128)} %refs_0_.1) | copy-start | bytes 6291460
  36.4 78.1 %all-to-all-start = ((f32[128,4,128]{2,1,0:T(4,128)}), f32[128,4,128]{2,1,0:T(4,128)S(1)}, u32[]{:S(2)}, u32[]{:S(2)}) async-start(f32[128,4,128]{2,1,0:T(4,128)} %cells.1), calls=%async_computation | async-start | bytes 524288 | tf_op jit(solution)/shard_map/all_to_all | solution.py:291
  45.0 1.6 %copy-start.3 = (f32[32,128,128]{2,1,0:T(8,128)S(1)}, f32[32,128,128]{2,1,0:T(8,128)}, u32[]{:S(2)}) copy-start(f32[32,128,128]{2,1,0:T(8,128)} %refs_0_.1) | copy-start | bytes 6291460
  46.6 1.6 %copy-start.4 = (f32[32,128,128]{2,1,0:T(8,128)S(1)}, f32[32,128,128]{2,1,0:T(8,128)}, u32[]{:S(2)}) copy-start(f32[32,128,128]{2,1,0:T(8,128)} %refs_2_.1) | copy-start | bytes 6291460
  59.3 8.8 %collective-permute-start.5 = (f32[1,128,128]{2,1,0:T(8,128)S(1)}, f32[1,128,128]{2,1,0:T(8,128)S(1)}, u32[]{:S(2)}, u32[]{:S(2)}) collective-permute-start(f32[1,128,128]{2,1,0:T(8,128)S(1)} %get-tuple-element.29), channel_id=1, source_target_pairs={{0,8},{8,16},{16,24},{24,0},{1,9},{9,17},{17,25},{25,1},{2,10},{10... | collective-permute-start | bytes 196616 | tf_op jit(solution)/shard_map/ppermute | solution.py:216
  61.1 7.0 %collective-permute-start.6 = (f32[1,128,128]{2,1,0:T(8,128)S(1)}, f32[1,128,128]{2,1,0:T(8,128)S(1)}, u32[]{:S(2)}, u32[]{:S(2)}) collective-permute-start(f32[1,128,128]{2,1,0:T(8,128)S(1)} %get-tuple-element.30), channel_id=1, source_target_pairs={{8,0},{16,8},{24,16},{0,24},{9,1},{17,9},{25,17},{1,25},{10,2},{18... | collective-permute-start | bytes 196616 | tf_op jit(solution)/shard_map/ppermute | solution.py:217
  63.2 5.0 %collective-permute-start.9 = (f32[2,4,8,128]{3,2,1,0:T(8,128)S(1)}, f32[2,4,8,128]{3,2,1,0:T(8,128)S(1)}, u32[]{:S(2)}, u32[]{:S(2)}) collective-permute-start(f32[2,4,8,128]{3,2,1,0:T(8,128)S(1)} %get-tuple-element.33), channel_id=1, source_target_pairs={{0,1},{1,0},{2,3},{3,2},{4,5},{5,4},{6,7},{7,6},{8,9},{9,8},{10,11... | collective-permute-start | bytes 98312 | tf_op jit(solution)/shard_map/ppermute | solution.py:221
  64.9 3.2 %collective-permute-start.7 = (f32[32,128]{1,0:T(8,128)S(1)}, f32[32,128]{1,0:T(8,128)S(1)}, u32[]{:S(2)}, u32[]{:S(2)}) collective-permute-start(f32[32,128]{1,0:T(8,128)S(1)} %get-tuple-element.31), channel_id=1, source_target_pairs={{0,2},{2,4},{4,6},{6,0},{1,3},{3,5},{5,7},{7,1},{8,10},{10,12},{12... | collective-permute-start | bytes 49160 | tf_op jit(solution)/shard_map/ppermute | solution.py:218
  64.9 3.2 %collective-permute-start.8 = (f32[32,128]{1,0:T(8,128)S(1)}, f32[32,128]{1,0:T(8,128)S(1)}, u32[]{:S(2)}, u32[]{:S(2)}) collective-permute-start(f32[32,128]{1,0:T(8,128)S(1)} %get-tuple-element.32), channel_id=1, source_target_pairs={{2,0},{4,2},{6,4},{0,6},{3,1},{5,3},{7,5},{1,7},{10,8},{12,10},{14... | collective-permute-start | bytes 49160 | tf_op jit(solution)/shard_map/ppermute | solution.py:219
  79.3 8.1 %collective-permute-start.10 = (f32[1,128,128]{2,1,0:T(8,128)S(1)}, f32[1,128,128]{2,1,0:T(8,128)S(1)}, u32[]{:S(2)}, u32[]{:S(2)}) collective-permute-start(f32[1,128,128]{2,1,0:T(8,128)S(1)} %get-tuple-element.35), channel_id=1, source_target_pairs={{0,8},{8,16},{16,24},{24,0},{1,9},{9,17},{17,25},{25,1},{2,10},{10... | collective-permute-start | bytes 196616 | tf_op jit(solution)/shard_map/ppermute | solution.py:216
  79.3 8.1 %collective-permute-start.11 = (f32[1,128,128]{2,1,0:T(8,128)S(1)}, f32[1,128,128]{2,1,0:T(8,128)S(1)}, u32[]{:S(2)}, u32[]{:S(2)}) collective-permute-start(f32[1,128,128]{2,1,0:T(8,128)S(1)} %get-tuple-element.36), channel_id=1, source_target_pairs={{8,0},{16,8},{24,16},{0,24},{9,1},{17,9},{25,17},{1,25},{10,2},{18... | collective-permute-start | bytes 196616 | tf_op jit(solution)/shard_map/ppermute | solution.py:217
  83.1 4.2 %collective-permute-start.14 = (f32[2,4,8,128]{3,2,1,0:T(8,128)S(1)}, f32[2,4,8,128]{3,2,1,0:T(8,128)S(1)}, u32[]{:S(2)}, u32[]{:S(2)}) collective-permute-start(f32[2,4,8,128]{3,2,1,0:T(8,128)S(1)} %get-tuple-element.39), channel_id=1, source_target_pairs={{0,1},{1,0},{2,3},{3,2},{4,5},{5,4},{6,7},{7,6},{8,9},{9,8},{10,11... | collective-permute-start | bytes 98312 | tf_op jit(solution)/shard_map/ppermute | solution.py:221
  83.8 3.2 %collective-permute-start.12 = (f32[32,128]{1,0:T(8,128)S(1)}, f32[32,128]{1,0:T(8,128)S(1)}, u32[]{:S(2)}, u32[]{:S(2)}) collective-permute-start(f32[32,128]{1,0:T(8,128)S(1)} %get-tuple-element.37), channel_id=1, source_target_pairs={{0,2},{2,4},{4,6},{6,0},{1,3},{3,5},{5,7},{7,1},{8,10},{10,12},{12... | collective-permute-start | bytes 49160 | tf_op jit(solution)/shard_map/ppermute | solution.py:218
  84.4 2.6 %collective-permute-start.13 = (f32[32,128]{1,0:T(8,128)S(1)}, f32[32,128]{1,0:T(8,128)S(1)}, u32[]{:S(2)}, u32[]{:S(2)}) collective-permute-start(f32[32,128]{1,0:T(8,128)S(1)} %get-tuple-element.38), channel_id=1, source_target_pairs={{2,0},{4,2},{6,4},{0,6},{3,1},{5,3},{7,5},{1,7},{10,8},{12,10},{14... | collective-permute-start | bytes 49160 | tf_op jit(solution)/shard_map/ppermute | solution.py:219
  98.5 8.0 %collective-permute-start.15 = (f32[1,128,128]{2,1,0:T(8,128)S(1)}, f32[1,128,128]{2,1,0:T(8,128)S(1)}, u32[]{:S(2)}, u32[]{:S(2)}) collective-permute-start(f32[1,128,128]{2,1,0:T(8,128)S(1)} %get-tuple-element.41), channel_id=1, source_target_pairs={{0,8},{8,16},{16,24},{24,0},{1,9},{9,17},{17,25},{25,1},{2,10},{10... | collective-permute-start | bytes 196616 | tf_op jit(solution)/shard_map/ppermute | solution.py:216
  98.5 8.0 %collective-permute-start.16 = (f32[1,128,128]{2,1,0:T(8,128)S(1)}, f32[1,128,128]{2,1,0:T(8,128)S(1)}, u32[]{:S(2)}, u32[]{:S(2)}) collective-permute-start(f32[1,128,128]{2,1,0:T(8,128)S(1)} %get-tuple-element.42), channel_id=1, source_target_pairs={{8,0},{16,8},{24,16},{0,24},{9,1},{17,9},{25,17},{1,25},{10,2},{18... | collective-permute-start | bytes 196616 | tf_op jit(solution)/shard_map/ppermute | solution.py:217
  102.3 4.2 %collective-permute-start.19 = (f32[2,4,8,128]{3,2,1,0:T(8,128)S(1)}, f32[2,4,8,128]{3,2,1,0:T(8,128)S(1)}, u32[]{:S(2)}, u32[]{:S(2)}) collective-permute-start(f32[2,4,8,128]{3,2,1,0:T(8,128)S(1)} %get-tuple-element.45), channel_id=1, source_target_pairs={{0,1},{1,0},{2,3},{3,2},{4,5},{5,4},{6,7},{7,6},{8,9},{9,8},{10,11... | collective-permute-start | bytes 98312 | tf_op jit(solution)/shard_map/ppermute | solution.py:221
  103.3 3.2 %collective-permute-start.17 = (f32[32,128]{1,0:T(8,128)S(1)}, f32[32,128]{1,0:T(8,128)S(1)}, u32[]{:S(2)}, u32[]{:S(2)}) collective-permute-start(f32[32,128]{1,0:T(8,128)S(1)} %get-tuple-element.43), channel_id=1, source_target_pairs={{0,2},{2,4},{4,6},{6,0},{1,3},{3,5},{5,7},{7,1},{8,10},{10,12},{12... | collective-permute-start | bytes 49160 | tf_op jit(solution)/shard_map/ppermute | solution.py:218
  104.0 2.5 %collective-permute-start.18 = (f32[32,128]{1,0:T(8,128)S(1)}, f32[32,128]{1,0:T(8,128)S(1)}, u32[]{:S(2)}, u32[]{:S(2)}) collective-permute-start(f32[32,128]{1,0:T(8,128)S(1)} %get-tuple-element.44), channel_id=1, source_target_pairs={{2,0},{4,2},{6,4},{0,6},{3,1},{5,3},{7,5},{1,7},{10,8},{12,10},{14... | collective-permute-start | bytes 49160 | tf_op jit(solution)/shard_map/ppermute | solution.py:219

commit v2 on v1

v2 whole, which is shorter than its diff:
```python
import functools

import jax
import jax.numpy as jnp
from jax import lax
from jax.experimental import pallas as pl
from jax.experimental.pallas import tpu as pltpu
from jax.sharding import PartitionSpec as P

ITERS = 4
CAP = 4
LANES = 128
SUBLANES = 8
GAUSS_RATE = 0.5
AXES = ("fx", "fy", "fz")
F32 = jnp.float32


def vmem():
    return pl.BlockSpec(memory_space=pltpu.VMEM)


def hbm():
    return pl.BlockSpec(memory_space=pltpu.HBM)


def smem():
    return pl.BlockSpec(memory_space=pltpu.SMEM)


def params(mib):
    return pltpu.CompilerParams(vmem_limit_bytes=mib * 1024 * 1024)


def shape_of(*dims):
    return jax.ShapeDtypeStruct(dims, F32)


def z_pack_dims(cx, cy):
    per = cy // SUBLANES
    planes = LANES // per
    return per, planes, cx // planes


def edge_z(side, plane, offset, packed, lane):
    col = 0 if side == 0 else LANES - 1
    for j in range(plane.shape[0] // SUBLANES):
        part = plane[j * SUBLANES : (j + 1) * SUBLANES, col : col + 1]
        spread = jnp.broadcast_to(part, (SUBLANES, LANES))
        packed = spread if packed is None else jnp.where(lane == offset + j, spread, packed)
    return packed


def column_z(packed, offset, per):
    parts = [
        jnp.broadcast_to(packed[:, offset + j : offset + j + 1], (SUBLANES, LANES))
        for j in range(per)
    ]
    return jnp.concatenate(parts, axis=0)


def emit_y(plane, x, ylo_ref, yhi_ref):
    ylo_ref[pl.ds(x, 1), :] = plane[0:1]
    yhi_ref[pl.ds(x, 1), :] = plane[plane.shape[0] - 1 :]


def faces_kernel(p_ref, copy_ref, xlo_ref, xhi_ref, ylo_ref, yhi_ref, zf_ref):
    cx, cy, _ = p_ref.shape
    per, planes, packs = z_pack_dims(cx, cy)
    lane = lax.broadcasted_iota(jnp.int32, (SUBLANES, LANES), 1)
    xlo_ref[0] = p_ref[0]
    xhi_ref[0] = p_ref[cx - 1]

    def step(block, carry):
        packed = [None, None]
        for u in range(planes):
            x = block * planes + u
            plane = p_ref[x]
            copy_ref[x] = plane
            emit_y(plane, x, ylo_ref, yhi_ref)
            for side in range(2):
                packed[side] = edge_z(side, plane, u * per, packed[side], lane)
        zf_ref[0, block] = packed[0]
        zf_ref[1, block] = packed[1]
        return carry

    lax.fori_loop(0, packs, step, 0)


def sweep_kernel(first, last, swap, *refs):
    p_ref, src_ref, inv_in_ref, xlo_ref, xhi_ref, ylo_ref, yhi_ref, zr_ref = refs[:8]
    outs = refs[8:]
    out_ref = outs[0]
    outs = outs[1:]
    if first:
        inv_out_ref = outs[0]
        outs = outs[1:]
    cx, cy, cz = p_ref.shape
    per, planes, packs = z_pack_dims(cx, cy)
    zlo_at, zhi_at = (1, 0) if swap else (0, 1)
    if not last:
        xlo_out, xhi_out, ylo_out, yhi_out, zf_ref = outs
    lane = lax.broadcasted_iota(jnp.int32, (cy, cz), 1)
    small_lane = lax.broadcasted_iota(jnp.int32, (SUBLANES, LANES), 1)

    def step(block, carry):
        packed = [None, None]
        zlo_pack = zr_ref[zlo_at, block]
        zhi_pack = zr_ref[zhi_at, block]
        for u in range(planes):
            x = block * planes + u
            if u == 0:
                below = jnp.where(block == 0, xlo_ref[0], p_ref[jnp.maximum(x - 1, 0)])
            else:
                below = p_ref[x - 1]
            if u == planes - 1:
                above = jnp.where(block == packs - 1, xhi_ref[0], p_ref[jnp.minimum(x + 1, cx - 1)])
            else:
                above = p_ref[x + 1]
            here = p_ref[x]
            total = below + above
            total = total + jnp.concatenate([ylo_ref[pl.ds(x, 1), :], here[: cy - 1]], axis=0)
            total = total + jnp.concatenate([here[1:], yhi_ref[pl.ds(x, 1), :]], axis=0)
            zlo = column_z(zlo_pack, u * per, per)
            zhi = column_z(zhi_pack, u * per, per)
            total = total + jnp.where(lane == 0, zlo, pltpu.roll(here, 1, 1))
            total = total + jnp.where(lane == cz - 1, zhi, pltpu.roll(here, cz - 1, 1))
            if first:
                inv = 1.0 / (6.0 + inv_in_ref[x])
                inv_out_ref[x] = inv
            else:
                inv = inv_in_ref[x]
            result = (total + src_ref[x]) * inv
            out_ref[x] = result
            if not last:
                emit_y(result, x, ylo_out, yhi_out)
                for side in range(2):
                    packed[side] = edge_z(side, result, u * per, packed[side], small_lane)
        if not last:
            zf_ref[0, block] = packed[0]
            zf_ref[1, block] = packed[1]
        return carry

    lax.fori_loop(0, packs, step, 0)
    if not last:
        xlo_out[0] = out_ref[0]
        xhi_out[0] = out_ref[cx - 1]


FAR = 100.0


def gather_kernel(
    row_ref, target_ref, p_ref, lane_ref, coef_ref, xyz_ref, src_ref, diag_ref,
    out_ref, src_out, diag_out, sems,
):
    copies = [
        pltpu.make_async_copy(src_ref, src_out, sems.at[0]),
        pltpu.make_async_copy(diag_ref, diag_out, sems.at[1]),
    ]
    for copy in copies:
        copy.start()
    tiles, width = coef_ref.shape
    out_ref[...] = jnp.full(out_ref.shape, FAR, F32)
    sub = lax.broadcasted_iota(jnp.int32, (SUBLANES, LANES), 0)
    lane = lax.broadcasted_iota(jnp.int32, (SUBLANES, LANES), 1)

    def one_tile(t):
        pick = jnp.broadcast_to(lane_ref[pl.ds(t, 1), :], (SUBLANES, LANES))
        total = jnp.zeros((SUBLANES, LANES), F32)
        for group in range(width // SUBLANES):
            rows = None
            for s in range(SUBLANES):
                at = row_ref[t, group * SUBLANES + s]
                row = jnp.broadcast_to(p_ref[pl.ds(at, 1), :], (SUBLANES, LANES))
                rows = row if rows is None else jnp.where(sub == s, row, rows)
            picked = jnp.take_along_axis(rows, pick, axis=1, mode="promise_in_bounds")
            total = jnp.where(lane == sub + group * SUBLANES, picked, total)
        values = jnp.sum(total, axis=0, keepdims=True) * coef_ref[pl.ds(t, 1), :]
        slot = target_ref[t]
        out_ref[slot, 0:1, :] = values
        for c in range(3):
            out_ref[slot, c + 1 : c + 2, :] = xyz_ref[c, pl.ds(t, 1), :]

    def tile_step(pair, carry):
        one_tile(pair * 2)
        one_tile(pair * 2 + 1)
        return carry

    lax.fori_loop(0, tiles // 2, tile_step, 0)
    for copy in copies:
        copy.wait()


def lane_gather(row, chunks, low, high):
    got = None
    for at in range(chunks):
        part = jnp.broadcast_to(row[:, at * LANES : (at + 1) * LANES], (SUBLANES, LANES))
        part = jnp.take_along_axis(part, low, axis=1, mode="promise_in_bounds")
        got = part if got is None else jnp.where(high == at, part, got)
    return got


def node_kernel(inc_ref, wanted_ref, node_ref, out_ref, table_ref):
    slots = inc_ref.shape[0]
    width = inc_ref.shape[2]
    neigh, rows, _ = wanted_ref.shape
    chunks = slots // LANES
    scale = GAUSS_RATE ** 0.5
    for c in range(4):
        part = inc_ref[:, c, :]
        if c > 0:
            part = part * scale
        table_ref[c] = part.T
    half = 0.5 * FAR * scale
    row_id = lax.broadcasted_iota(jnp.int32, (slots, slots), 0).astype(F32)
    col_id = lax.broadcasted_iota(jnp.int32, (slots, slots), 1).astype(F32)
    first_row = table_ref[1, 0:1, :]
    used_row = jnp.broadcast_to(jnp.where(first_row < half, 1.0, 0.0), (slots, slots))
    used_col = jnp.where(inc_ref[:, 1, :][:, 0:1] < 0.5 * FAR, 1.0, 0.0)
    prefix = jnp.sum(jnp.where(col_id <= row_id, used_row, 0.0), axis=1, keepdims=True)
    count = jnp.max(prefix, axis=0, keepdims=True)
    place = jnp.where(prefix == col_id + 1.0, row_id, 0.0) * used_col
    slot_row = jnp.sum(place, axis=0, keepdims=True).astype(jnp.int32)
    count = jnp.broadcast_to(count, (SUBLANES, LANES))
    ratio = 1.0 / count
    span = 128 // chunks

    def pair(step, carry):
        k = step % neigh
        block = step // neigh
        at = pl.ds(pl.multiple_of(block * SUBLANES, SUBLANES), SUBLANES)
        listed = wanted_ref[k, at, :].astype(F32)
        rest = listed - jnp.floor(listed * ratio) * count
        rest = jnp.where(rest < 0.0, rest + count, rest)
        rest = jnp.where(rest >= count, rest - count, rest)
        wanted = rest.astype(jnp.int32)
        chosen = lane_gather(slot_row, chunks, wanted % LANES, wanted // LANES)
        low = chosen % LANES
        high = chosen // LANES
        coords = [node_ref[c, at, :] * scale for c in range(3)]
        before = jnp.where(k == 0, 0.0, out_ref[at, :])

        def points(base, total):
            sums = [total, None, None, None]
            for u in range(span):
                p = base * span + u
                got = [
                    lane_gather(table_ref[c, pl.ds(p, 1), :], chunks, low, high) for c in range(4)
                ]
                gaps = [coords[c] - got[c + 1] for c in range(3)]
                dist = gaps[0] * gaps[0] + gaps[1] * gaps[1] + gaps[2] * gaps[2]
                term = jnp.exp(-dist) * got[0]
                sums[u % 4] = term if sums[u % 4] is None else sums[u % 4] + term
            return (sums[0] + sums[1]) + (sums[2] + sums[3])

        if width == span:
            out_ref[at, :] = points(0, before)
        else:
            out_ref[at, :] = lax.fori_loop(0, width // span, points, before)
        return carry

    lax.fori_loop(0, neigh * (rows // SUBLANES), pair, 0)


def ring(axis, up):
    count = lax.axis_size(axis)
    if up:
        return [(i, (i + 1) % count) for i in range(count)]
    return [((i + 1) % count, i) for i in range(count)]


def exchange(xlo, xhi, ylo, yhi, zf):
    from_x_lo = lax.ppermute(xhi, "fx", ring("fx", True))
    from_x_hi = lax.ppermute(xlo, "fx", ring("fx", False))
    from_y_lo = lax.ppermute(yhi, "fy", ring("fy", True))
    from_y_hi = lax.ppermute(ylo, "fy", ring("fy", False))
    if lax.axis_size("fz") == 2:
        z = lax.ppermute(zf, "fz", ring("fz", True))
    else:
        z = jnp.stack(
            [
                lax.ppermute(zf[1], "fz", ring("fz", True)),
                lax.ppermute(zf[0], "fz", ring("fz", False)),
            ]
        )
    return from_x_lo, from_x_hi, from_y_lo, from_y_hi, z


def on_device(
    pressure, source, diag_shift, iface_cells, iface_coef, iface_xyz, node_xyz, owners, node_lists
):
    devices = lax.axis_size(AXES)
    cx, cy, cz = pressure.shape
    tiles_dev = owners.shape[0]
    width = iface_coef.shape[0] // tiles_dev
    node_count, neigh = node_lists.shape
    slots = devices * CAP
    per, planes, packs = z_pack_dims(cx, cy)
    y_shape = shape_of(cx, cz)
    z_shape = shape_of(2, packs, SUBLANES, LANES)
    x_shape = shape_of(1, cy, cz)
    block = shape_of(cx, cy, cz)

    order = lax.broadcasted_iota(jnp.int32, (tiles_dev, tiles_dev), 0)
    other = lax.broadcasted_iota(jnp.int32, (tiles_dev, tiles_dev), 1)
    same = (owners[:, None] == owners[None, :]) & (other < order)
    target = owners * CAP + jnp.sum(same.astype(jnp.int32), axis=1)
    listed = node_lists.T.reshape(neigh, node_count // LANES, LANES)

    current, *faces = pl.pallas_call(
        faces_kernel,
        out_shape=(block, x_shape, x_shape, y_shape, y_shape, z_shape),
        in_specs=[vmem()],
        out_specs=(vmem(),) * 6,
        compiler_params=params(8),
        name="faces",
    )(pressure)
    halos = exchange(*faces)

    outgoing, source_near, inverse = pl.pallas_call(
        gather_kernel,
        out_shape=(shape_of(slots, 4, width), block, block),
        in_specs=[smem(), smem(), vmem(), vmem(), vmem(), vmem(), hbm(), hbm()],
        out_specs=(vmem(),) * 3,
        scratch_shapes=[pltpu.SemaphoreType.DMA((2,))],
        compiler_params=params(16),
        name="cells",
    )(
        (iface_cells // cz).reshape(tiles_dev, width),
        target,
        current.reshape(cx * cy, cz),
        (iface_cells % cz).reshape(tiles_dev, width),
        iface_coef.reshape(tiles_dev, width),
        iface_xyz.reshape(3, tiles_dev, width),
        source,
        diag_shift,
    )
    incoming = lax.all_to_all(outgoing, AXES, split_axis=0, concat_axis=0, tiled=True)

    swap = lax.axis_size("fz") == 2
    for index in range(ITERS):
        first, last = index == 0, index == ITERS - 1
        shapes = [block]
        if first:
            shapes.append(block)
        if not last:
            shapes += [x_shape, x_shape, y_shape, y_shape, z_shape]
        results = pl.pallas_call(
            functools.partial(sweep_kernel, first, last, swap),
            out_shape=tuple(shapes),
            in_specs=[vmem()] * 8,
            out_specs=tuple(vmem() for _ in shapes),
            compiler_params=params(16),
            name="sweep",
        )(current, source_near, inverse, *halos)
        current = results[0]
        if first:
            inverse = results[1]
        if not last:
            halos = exchange(*results[-5:])

    loads = pl.pallas_call(
        node_kernel,
        out_shape=shape_of(node_count // LANES, LANES),
        in_specs=[vmem()] * 3,
        out_specs=vmem(),
        scratch_shapes=[pltpu.VMEM((4, width, slots), F32)],
        compiler_params=params(12),
        name="nodes",
    )(incoming, listed, node_xyz.reshape(3, node_count // LANES, LANES))
    return current, loads.reshape(node_count)


def solution(mesh):
    placed = (
        P("fx", "fy", "fz"),
        P("fx", "fy", "fz"),
        P("fx", "fy", "fz"),
        P(AXES),
        P(AXES),
        P(None, AXES),
        P(None, AXES),
        P(AXES),
        P(AXES, None),
    )
    return jax.shard_map(
        on_device,
        mesh=mesh,
        in_specs=placed,
        out_specs=(P("fx", "fy", "fz"), P(AXES)),
        check_vma=False,
    )
```

time: 137 us -> 104 us (0.76)
  Pallas kernels: 81 us -> 49.1 us
  waiting for transfers between devices: 4.38 us -> 8.1 us
  starting transfers between devices: 37.7 us -> 34.8 us
  other arithmetic: 2.66 us -> 1 us
  local copies, waits for them, and re-layouts: 7.39 us -> 8.79 us
    pallas_call x4, Pallas kernels: 41.4 us -> 23.5 us  [on_device(): pl.pallas_call(functools.partial(sweep_kernel, first, last, swap), out_sh...]
    pallas_call x1, Pallas kernels: 20.8 us -> 13.2 us  [on_device(): pl.pallas_call(node_kernel, out_shape=shape_of(node_count // LANES, LANES...]
    pallas_call x2, Pallas kernels: 18.7 us -> 12.4 us  [the longest x1 11 us: on_device(): pl.pallas_call(gather_kernel, out_shape=(shape_of(slots, 4, width), block...]
    all_to_all x1 -> x0, starting transfers between devices: 3.1 us -> none  [on_device(): lax.all_to_all(filled, AXES, split_axis=0, concat_axis=0, tiled=True)]
    unnamed x25, local copies, waits for them, and re-layouts: 6.41 us -> 8.79 us
    ppermute x4, waiting for transfers between devices: 0.01 us -> 2.04 us  [exchange(): from_x_lo = lax.ppermute(xhi, 'fx', ring('fx', True))]
    ppermute x4, waiting for transfers between devices: 3.94 us -> 5.63 us  [exchange(): from_y_lo = lax.ppermute(yhi, 'fy', ring('fy', True))]
    all_to_all x1, starting transfers between devices: 5.83 us -> 7.33 us  [on_device(): lax.all_to_all(outgoing, AXES, split_axis=0, concat_axis=0, tiled=True)]
  transfers between devices with their start and end apart: 22 -> 21, of which waited for: 4 -> 6; matrix products, arithmetic and copies ran while one was open for 3% -> 0% of each run, Pallas kernels for 40% -> 23%
where the time goes in v2:
time: 104 us; the launch traced here: 103 us
  Pallas kernels  49.1 us (47%)
  starting transfers between devices  34.8 us (33%)
  local copies, waits for them, and re-layouts  8.79 us (8%)
  waiting for transfers between devices  8.1 us (8%)
    pallas_call x4, Pallas kernels, on_device(): pl.pallas_call(functools.partial(sweep_kernel, first, last, swap), out_sh...  23.5 us
    pallas_call x1, Pallas kernels, on_device(): pl.pallas_call(node_kernel, out_shape=shape_of(node_count // LANES, LANES...  13.2 us
    ppermute x4, starting transfers between devices, exchange(): from_x_hi = lax.ppermute(xlo, 'fx', ring('fx', False))  11.6 us
    pallas_call x1, Pallas kernels, on_device(): pl.pallas_call(gather_kernel, out_shape=(shape_of(slots, 4, width), block...  11 us
    unnamed x25, local copies, waits for them, and re-layouts  8.79 us
    all_to_all x1, starting transfers between devices, on_device(): lax.all_to_all(outgoing, AXES, split_axis=0, concat_axis=0, tiled=True)  7.33 us
    ppermute x4, starting transfers between devices, exchange(): from_y_hi = lax.ppermute(ylo, 'fy', ring('fy', False))  5.71 us
    ppermute x4, waiting for transfers between devices, exchange(): from_y_lo = lax.ppermute(yhi, 'fy', ring('fy', True))  5.63 us
  transfers between devices with their start and end apart: 21, of which 6 were waited for; matrix products, arithmetic and copies ran while one was open for 0% of the time, Pallas kernels for 23%

profile of v2, /device:TPU:0, one launch (start us, length us, event | category | flops | bytes accessed | tf_op | source)
XLA Modules:
  0.0 102.6 jit_solution(10441189113970530796)
XLA Ops:
  0.6 0.0 copy-start.2
  0.6 0.0 copy-start.6
  0.7 1.7 %copy-done.6 = f32[32,128,128]{2,1,0:T(8,128)S(1)} copy-done((f32[32,128,128]{2,1,0:T(8,128)S(1)}, f32[32,128,128]{2,1,0:T(8,128)}, u32[]{:S(2)}) %copy-start.6) | copy-done | bytes 2097176
  2.4 1.4 %faces.1 = (f32[32,128,128]{2,1,0:T(8,128)S(1)}, f32[1,128,128]{2,1,0:T(8,128)S(1)}, f32[1,128,128]{2,1,0:T(8,128)S(1)}, f32[32,128]{1,0:T(8,128)S(1)}, f32[32,1...) custom-call(f32[32,128,128]{2,1,0:T(8,128)S(1)} %copy-done.6), custom_call_target="tpu_custom_call" | custom-call | tf_op jit(solution)/shard_map/faces/pallas_call | solution.py:311
  3.8 0.0 copy-start
  3.9 0.8 fusion.1
  4.7 0.9 copy.17
  5.6 0.2 convert_reduce_fusion
  5.8 0.0 copy-done.2
  5.8 0.0 copy-done.7
  5.8 0.0 copy-start.3
  5.8 1.6 %copy-done.3 = f32[32,128,128]{2,1,0:T(8,128)S(1)} copy-done((f32[32,128,128]{2,1,0:T(8,128)S(1)}, f32[32,128,128]{2,1,0:T(8,128)}, u32[]{:S(2)}) %copy-start.3) | copy-done | bytes 2097176
  7.4 11.0 %cells.1 = (f32[128,4,128]{2,1,0:T(4,128)}, f32[32,128,128]{2,1,0:T(8,128)S(1)}, f32[32,128,128]{2,1,0:T(8,128)S(1)}) custom-call(s32[64,128]{1,0:T(8,128)S(1)} %get-tuple-element.59.row_ref, s32[64]{0:T(128)S(1)} %multiply_add_fusion.target_ref, f32[4096,128]{1,0:T(8,128)S(1)} %bitcast.20, s32[64,128]{1,0:T(8,128)S(1)} %get-tuple-element.58.lane_ref, ...), custom_call_target="tpu_custom_call" | custom-call | tf_op jit(solution)/shard_map/cells/pallas_call | solution.py:321
  18.4 1.3 %copy-done.4 = f32[32,128,128]{2,1,0:T(8,128)} copy-done((f32[32,128,128]{2,1,0:T(8,128)}, f32[32,128,128]{2,1,0:T(8,128)S(1)}, u32[]{:S(2)}) %copy-start.4) | copy-done | bytes 2097176
  19.7 7.3 %all-to-all-start = ((f32[128,4,128]{2,1,0:T(4,128)}), f32[128,4,128]{2,1,0:T(4,128)S(1)}, u32[]{:S(2)}, u32[]{:S(2)}) async-start(f32[128,4,128]{2,1,0:T(4,128)} %get-tuple-element.57), calls=%async_computation | async-start | bytes 524288 | tf_op jit(solution)/shard_map/all_to_all | solution.py:339
  27.0 1.8 %collective-permute-start = (f32[1,128,128]{2,1,0:T(8,128)S(1)}, f32[1,128,128]{2,1,0:T(8,128)S(1)}, u32[]{:S(2)}, u32[]{:S(2)}) collective-permute-start(f32[1,128,128]{2,1,0:T(8,128)S(1)} %get-tuple-element.33), channel_id=1, source_target_pairs={{0,8},{8,16},{16,24},{24,0},{1,9},{9,17},{17,25},{25,1},{2,10},{10... | collective-permute-start | bytes 196616 | tf_op jit(solution)/shard_map/ppermute | solution.py:274
  28.9 2.1 %collective-permute-start.1 = (f32[1,128,128]{2,1,0:T(8,128)S(1)}, f32[1,128,128]{2,1,0:T(8,128)S(1)}, u32[]{:S(2)}, u32[]{:S(2)}) collective-permute-start(f32[1,128,128]{2,1,0:T(8,128)S(1)} %get-tuple-element.34), channel_id=1, source_target_pairs={{8,0},{16,8},{24,16},{0,24},{9,1},{17,9},{25,17},{1,25},{10,2},{18... | collective-permute-start | bytes 196616 | tf_op jit(solution)/shard_map/ppermute | solution.py:275
  30.9 1.8 %collective-permute-start.4 = (f32[2,4,8,128]{3,2,1,0:T(8,128)S(1)}, f32[2,4,8,128]{3,2,1,0:T(8,128)S(1)}, u32[]{:S(2)}, u32[]{:S(2)}) collective-permute-start(f32[2,4,8,128]{3,2,1,0:T(8,128)S(1)} %get-tuple-element.37), channel_id=1, source_target_pairs={{0,1},{1,0},{2,3},{3,2},{4,5},{5,4},{6,7},{7,6},{8,9},{9,8},{10,11... | collective-permute-start | bytes 98312 | tf_op jit(solution)/shard_map/ppermute | solution.py:279
  32.7 0.0 collective-permute-start.2
  32.7 1.7 %collective-permute-start.3 = (f32[32,128]{1,0:T(8,128)S(1)}, f32[32,128]{1,0:T(8,128)S(1)}, u32[]{:S(2)}, u32[]{:S(2)}) collective-permute-start(f32[32,128]{1,0:T(8,128)S(1)} %get-tuple-element.36), channel_id=1, source_target_pairs={{2,0},{4,2},{6,4},{0,6},{3,1},{5,3},{7,5},{1,7},{10,8},{12,10},{14... | collective-permute-start | bytes 49160 | tf_op jit(solution)/shard_map/ppermute | solution.py:277
  34.4 1.4 %collective-permute-done.2.refs_5_ = f32[32,128]{1,0:T(8,128)S(1)} collective-permute-done((f32[32,128]{1,0:T(8,128)S(1)}, f32[32,128]{1,0:T(8,128)S(1)}, u32[]{:S(2)}, u32[]{:S(2)}) %collective-permute-start.2) | collective-permute-done | bytes 16416 | tf_op jit(solution)/shard_map/ppermute | solution.py:276
  35.9 0.0 collective-permute-done.3.refs_6_
  35.9 0.0 collective-permute-done.4.refs_7_
  35.9 2.0 %collective-permute-done.refs_3_ = f32[1,128,128]{2,1,0:T(8,128)S(1)} collective-permute-done((f32[1,128,128]{2,1,0:T(8,128)S(1)}, f32[1,128,128]{2,1,0:T(8,128)S(1)}, u32[]{:S(2)}, u32[]{:S(2)}) %collective-permute-start) | collective-permute-done | bytes 65568 | tf_op jit(solution)/shard_map/ppermute | solution.py:274
  37.9 0.0 collective-permute-done.1.refs_4_
  37.9 1.6 %copy-done.1 = f32[32,128,128]{2,1,0:T(8,128)S(1)} copy-done((f32[32,128,128]{2,1,0:T(8,128)S(1)}, f32[32,128,128]{2,1,0:T(8,128)}, u32[]{:S(2)}) %copy-start.1) | copy-done | bytes 2097176
  39.5 1.6 %copy-done.5 = f32[32,128,128]{2,1,0:T(8,128)S(1)} copy-done((f32[32,128,128]{2,1,0:T(8,128)S(1)}, f32[32,128,128]{2,1,0:T(8,128)}, u32[]{:S(2)}) %copy-start.5) | copy-done | bytes 2097176
  41.1 6.3 %sweep.4 = (f32[32,128,128]{2,1,0:T(8,128)S(1)}, f32[32,128,128]{2,1,0:T(8,128)S(1)}, f32[1,128,128]{2,1,0:T(8,128)S(1)}, f32[1,128,128]{2,1,0:T(8,128)S(1)}, f3...) custom-call(f32[32,128,128]{2,1,0:T(8,128)S(1)} %copy-done.1, ...), custom_call_target="tpu_custom_call" | custom-call | tf_op jit(solution)/shard_map/sweep/pallas_call | solution.py:349
  47.4 1.9 %collective-permute-start.5 = (f32[1,128,128]{2,1,0:T(8,128)S(1)}, f32[1,128,128]{2,1,0:T(8,128)S(1)}, u32[]{:S(2)}, u32[]{:S(2)}) collective-permute-start(f32[1,128,128]{2,1,0:T(8,128)S(1)} %get-tuple-element.40), channel_id=1, source_target_pairs={{0,8},{8,16},{16,24},{24,0},{1,9},{9,17},{17,25},{25,1},{2,10},{10... | collective-permute-start | bytes 196616 | tf_op jit(solution)/shard_map/ppermute | solution.py:274
  49.3 2.0 %collective-permute-start.6 = (f32[1,128,128]{2,1,0:T(8,128)S(1)}, f32[1,128,128]{2,1,0:T(8,128)S(1)}, u32[]{:S(2)}, u32[]{:S(2)}) collective-permute-start(f32[1,128,128]{2,1,0:T(8,128)S(1)} %get-tuple-element.41), channel_id=1, source_target_pairs={{8,0},{16,8},{24,16},{0,24},{9,1},{17,9},{25,17},{1,25},{10,2},{18... | collective-permute-start | bytes 196616 | tf_op jit(solution)/shard_map/ppermute | solution.py:275
  51.3 1.5 %collective-permute-start.9 = (f32[2,4,8,128]{3,2,1,0:T(8,128)S(1)}, f32[2,4,8,128]{3,2,1,0:T(8,128)S(1)}, u32[]{:S(2)}, u32[]{:S(2)}) collective-permute-start(f32[2,4,8,128]{3,2,1,0:T(8,128)S(1)} %get-tuple-element.44), channel_id=1, source_target_pairs={{0,1},{1,0},{2,3},{3,2},{4,5},{5,4},{6,7},{7,6},{8,9},{9,8},{10,11... | collective-permute-start | bytes 98312 | tf_op jit(solution)/shard_map/ppermute | solution.py:279
  52.8 0.0 collective-permute-start.7
  52.8 1.7 %collective-permute-start.8 = (f32[32,128]{1,0:T(8,128)S(1)}, f32[32,128]{1,0:T(8,128)S(1)}, u32[]{:S(2)}, u32[]{:S(2)}) collective-permute-start(f32[32,128]{1,0:T(8,128)S(1)} %get-tuple-element.43), channel_id=1, source_target_pairs={{2,0},{4,2},{6,4},{0,6},{3,1},{5,3},{7,5},{1,7},{10,8},{12,10},{14... | collective-permute-start | bytes 49160 | tf_op jit(solution)/shard_map/ppermute | solution.py:277
  54.6 1.4 %collective-permute-done.7.refs_5_ = f32[32,128]{1,0:T(8,128)S(1)} collective-permute-done((f32[32,128]{1,0:T(8,128)S(1)}, f32[32,128]{1,0:T(8,128)S(1)}, u32[]{:S(2)}, u32[]{:S(2)}) %collective-permute-start.7) | collective-permute-done | bytes 16416 | tf_op jit(solution)/shard_map/ppermute | solution.py:276
  56.0 0.0 collective-permute-done.8.refs_6_
  56.0 0.0 collective-permute-done.9.refs_7_
  56.0 0.0 collective-permute-done.5.refs_3_
  56.0 0.0 collective-permute-done.6.refs_4_
  56.0 6.3 %sweep.5 = (f32[32,128,128]{2,1,0:T(8,128)S(1)}, f32[1,128,128]{2,1,0:T(8,128)S(1)}, f32[1,128,128]{2,1,0:T(8,128)S(1)}, f32[32,128]{1,0:T(8,128)S(1)}, f32[32,1...) custom-call(f32[32,128,128]{2,1,0:T(8,128)S(1)} %get-tuple-element.38.refs_0_, ...), custom_call_target="tpu_custom_call" | custom-call | tf_op jit(solution)/shard_map/sweep/pallas_call | solution.py:349
  62.4 0.1 collective-permute-start.10
  62.5 3.8 %collective-permute-start.11 = (f32[1,128,128]{2,1,0:T(8,128)S(1)}, f32[1,128,128]{2,1,0:T(8,128)S(1)}, u32[]{:S(2)}, u32[]{:S(2)}) collective-permute-start(f32[1,128,128]{2,1,0:T(8,128)S(1)} %get-tuple-element.47), channel_id=1, source_target_pairs={{8,0},{16,8},{24,16},{0,24},{9,1},{17,9},{25,17},{1,25},{10,2},{18... | collective-permute-start | bytes 196616 | tf_op jit(solution)/shard_map/ppermute | solution.py:275
  66.2 0.7 collective-permute-start.14
  67.0 0.5 collective-permute-start.12
  67.5 1.2 %collective-permute-start.13 = (f32[32,128]{1,0:T(8,128)S(1)}, f32[32,128]{1,0:T(8,128)S(1)}, u32[]{:S(2)}, u32[]{:S(2)}) collective-permute-start(f32[32,128]{1,0:T(8,128)S(1)} %get-tuple-element.49), channel_id=1, source_target_pairs={{2,0},{4,2},{6,4},{0,6},{3,1},{5,3},{7,5},{1,7},{10,8},{12,10},{14... | collective-permute-start | bytes 49160 | tf_op jit(solution)/shard_map/ppermute | solution.py:277
  68.7 1.4 %collective-permute-done.12.refs_5_ = f32[32,128]{1,0:T(8,128)S(1)} collective-permute-done((f32[32,128]{1,0:T(8,128)S(1)}, f32[32,128]{1,0:T(8,128)S(1)}, u32[]{:S(2)}, u32[]{:S(2)}) %collective-permute-start.12) | collective-permute-done | bytes 16416 | tf_op jit(solution)/shard_map/ppermute | solution.py:276
  70.1 0.0 collective-permute-done.13.refs_6_
  70.2 0.3 collective-permute-done.14.refs_7_
  70.5 0.0 collective-permute-done.10.refs_3_
  70.5 0.0 collective-permute-done.11.refs_4_
  70.5 0.0 copy-start.9
  70.5 6.3 %sweep.6 = (f32[32,128,128]{2,1,0:T(8,128)S(1)}, f32[1,128,128]{2,1,0:T(8,128)S(1)}, f32[1,128,128]{2,1,0:T(8,128)S(1)}, f32[32,128]{1,0:T(8,128)S(1)}, f32[32,1...) custom-call(f32[32,128,128]{2,1,0:T(8,128)S(1)} %get-tuple-element.45.refs_0_, ...), custom_call_target="tpu_custom_call" | custom-call | tf_op jit(solution)/shard_map/sweep/pallas_call | solution.py:349
  76.8 0.1 collective-permute-start.15
  76.9 3.8 %collective-permute-start.16 = (f32[1,128,128]{2,1,0:T(8,128)S(1)}, f32[1,128,128]{2,1,0:T(8,128)S(1)}, u32[]{:S(2)}, u32[]{:S(2)}) collective-permute-start(f32[1,128,128]{2,1,0:T(8,128)S(1)} %get-tuple-element.53), channel_id=1, source_target_pairs={{8,0},{16,8},{24,16},{0,24},{9,1},{17,9},{25,17},{1,25},{10,2},{18... | collective-permute-start | bytes 196616 | tf_op jit(solution)/shard_map/ppermute | solution.py:275
  80.7 1.0 collective-permute-start.19
  81.7 0.7 collective-permute-start.17
  82.4 1.0 collective-permute-start.18
  83.5 1.4 %collective-permute-done.17.refs_5_ = f32[32,128]{1,0:T(8,128)S(1)} collective-permute-done((f32[32,128]{1,0:T(8,128)S(1)}, f32[32,128]{1,0:T(8,128)S(1)}, u32[]{:S(2)}, u32[]{:S(2)}) %collective-permute-start.17) | collective-permute-done | bytes 16416 | tf_op jit(solution)/shard_map/ppermute | solution.py:276
  84.9 0.0 collective-permute-done.18.refs_6_
  84.9 0.0 collective-permute-done.19.refs_7_
  84.9 0.0 collective-permute-done.15.refs_3_
  84.9 0.0 collective-permute-done.16.refs_4_
  84.9 4.5 %sweep.7 = f32[32,128,128]{2,1,0:T(8,128)} custom-call(f32[32,128,128]{2,1,0:T(8,128)S(1)} %get-tuple-element.51.refs_0_, f32[32,128,128]{2,1,0:T(8,128)S(1)} %get-tuple-element.31.refs_1_, f32[32,128,128]{2,1,0:T(8,128)S(1)} %get-tuple-element.39.refs_2_, f32[1,128,128]{2,1,0:T(8,128)S(1)} %collective-permute-done.15.refs_3_, ...), custom_call_target="tpu_custom_call" | custom-call | tf_op jit(solution)/shard_map/sweep/pallas_call | solution.py:349
  89.5 0.0 all-to-all-done.inc_ref
  89.5 13.2 %nodes.1 = f32[16,128]{1,0:T(8,128)} custom-call(f32[128,4,128]{2,1,0:T(4,128)S(1)} %all-to-all-done.inc_ref, s32[8,16,128]{2,1,0:T(8,128)S(1)} %bitcast.22, f32[3,16,128]{2,1,0:T(8,128)S(1)} %bitcast.23), custom_call_target="tpu_custom_call" | custom-call | tf_op jit(solution)/shard_map/nodes/pallas_call | solution.py:363
  (13 shorter events, 0.0 us)
Async XLA Ops:
  0.6 5.1 %copy-start.2 = (f32[32,128,128]{2,1,0:T(8,128)S(1)}, f32[32,128,128]{2,1,0:T(8,128)}, u32[]{:S(2)}) copy-start(f32[32,128,128]{2,1,0:T(8,128)} %src_ref.1) | copy-start | bytes 6291460
  0.6 1.7 %copy-start.6 = (f32[32,128,128]{2,1,0:T(8,128)S(1)}, f32[32,128,128]{2,1,0:T(8,128)}, u32[]{:S(2)}) copy-start(f32[32,128,128]{2,1,0:T(8,128)} %p_ref.1) | copy-start | bytes 6291460
  2.4 3.2 %copy-start.10 = (s32[64]{0:T(128)S(1)}, s32[64]{0:T(128)}, u32[]{:S(2)}) copy-start(s32[64]{0:T(128)} %param.16) | copy-start | bytes 772
  2.4 3.4 %copy-start.7 = (f32[8192]{0:T(1024)S(1)}, f32[8192]{0:T(1024)}, u32[]{:S(2)}) copy-start(f32[8192]{0:T(1024)} %param.13) | copy-start | bytes 98308
  3.8 14.5 %copy-start = (f32[32,128,128]{2,1,0:T(8,128)}, f32[32,128,128]{2,1,0:T(8,128)S(1)}, u32[]{:S(2)}) copy-start(f32[32,128,128]{2,1,0:T(8,128)S(1)} %get-tuple-element.30.refs_0_) | copy-start | bytes 6291460
  5.8 1.6 %copy-start.3 = (f32[32,128,128]{2,1,0:T(8,128)S(1)}, f32[32,128,128]{2,1,0:T(8,128)}, u32[]{:S(2)}) copy-start(f32[32,128,128]{2,1,0:T(8,128)} %diag_ref.1) | copy-start | bytes 6291460
  18.4 1.3 %copy-start.4 = (f32[32,128,128]{2,1,0:T(8,128)}, f32[32,128,128]{2,1,0:T(8,128)S(1)}, u32[]{:S(2)}) copy-start(f32[32,128,128]{2,1,0:T(8,128)S(1)} %get-tuple-element.32.refs_2_) | copy-start | bytes 6291460
  19.7 69.8 %all-to-all-start = ((f32[128,4,128]{2,1,0:T(4,128)}), f32[128,4,128]{2,1,0:T(4,128)S(1)}, u32[]{:S(2)}, u32[]{:S(2)}) async-start(f32[128,4,128]{2,1,0:T(4,128)} %get-tuple-element.57), calls=%async_computation | async-start | bytes 524288 | tf_op jit(solution)/shard_map/all_to_all | solution.py:339
  27.0 10.9 %collective-permute-start = (f32[1,128,128]{2,1,0:T(8,128)S(1)}, f32[1,128,128]{2,1,0:T(8,128)S(1)}, u32[]{:S(2)}, u32[]{:S(2)}) collective-permute-start(f32[1,128,128]{2,1,0:T(8,128)S(1)} %get-tuple-element.33), channel_id=1, source_target_pairs={{0,8},{8,16},{16,24},{24,0},{1,9},{9,17},{17,25},{25,1},{2,10},{10... | collective-permute-start | bytes 196616 | tf_op jit(solution)/shard_map/ppermute | solution.py:274
  28.9 9.0 %collective-permute-start.1 = (f32[1,128,128]{2,1,0:T(8,128)S(1)}, f32[1,128,128]{2,1,0:T(8,128)S(1)}, u32[]{:S(2)}, u32[]{:S(2)}) collective-permute-start(f32[1,128,128]{2,1,0:T(8,128)S(1)} %get-tuple-element.34), channel_id=1, source_target_pairs={{8,0},{16,8},{24,16},{0,24},{9,1},{17,9},{25,17},{1,25},{10,2},{18... | collective-permute-start | bytes 196616 | tf_op jit(solution)/shard_map/ppermute | solution.py:275
  30.9 5.0 %collective-permute-start.4 = (f32[2,4,8,128]{3,2,1,0:T(8,128)S(1)}, f32[2,4,8,128]{3,2,1,0:T(8,128)S(1)}, u32[]{:S(2)}, u32[]{:S(2)}) collective-permute-start(f32[2,4,8,128]{3,2,1,0:T(8,128)S(1)} %get-tuple-element.37), channel_id=1, source_target_pairs={{0,1},{1,0},{2,3},{3,2},{4,5},{5,4},{6,7},{7,6},{8,9},{9,8},{10,11... | collective-permute-start | bytes 98312 | tf_op jit(solution)/shard_map/ppermute | solution.py:279
  32.7 3.2 %collective-permute-start.2 = (f32[32,128]{1,0:T(8,128)S(1)}, f32[32,128]{1,0:T(8,128)S(1)}, u32[]{:S(2)}, u32[]{:S(2)}) collective-permute-start(f32[32,128]{1,0:T(8,128)S(1)} %get-tuple-element.35), channel_id=1, source_target_pairs={{0,2},{2,4},{4,6},{6,0},{1,3},{3,5},{5,7},{7,1},{8,10},{10,12},{12... | collective-permute-start | bytes 49160 | tf_op jit(solution)/shard_map/ppermute | solution.py:276
  32.7 3.2 %collective-permute-start.3 = (f32[32,128]{1,0:T(8,128)S(1)}, f32[32,128]{1,0:T(8,128)S(1)}, u32[]{:S(2)}, u32[]{:S(2)}) collective-permute-start(f32[32,128]{1,0:T(8,128)S(1)} %get-tuple-element.36), channel_id=1, source_target_pairs={{2,0},{4,2},{6,4},{0,6},{3,1},{5,3},{7,5},{1,7},{10,8},{12,10},{14... | collective-permute-start | bytes 49160 | tf_op jit(solution)/shard_map/ppermute | solution.py:277
  37.9 1.6 %copy-start.1 = (f32[32,128,128]{2,1,0:T(8,128)S(1)}, f32[32,128,128]{2,1,0:T(8,128)}, u32[]{:S(2)}) copy-start(f32[32,128,128]{2,1,0:T(8,128)} %copy-done) | copy-start | bytes 6291460
  39.5 1.6 %copy-start.5 = (f32[32,128,128]{2,1,0:T(8,128)S(1)}, f32[32,128,128]{2,1,0:T(8,128)}, u32[]{:S(2)}) copy-start(f32[32,128,128]{2,1,0:T(8,128)} %copy-done.4) | copy-start | bytes 6291460
  47.4 8.6 %collective-permute-start.5 = (f32[1,128,128]{2,1,0:T(8,128)S(1)}, f32[1,128,128]{2,1,0:T(8,128)S(1)}, u32[]{:S(2)}, u32[]{:S(2)}) collective-permute-start(f32[1,128,128]{2,1,0:T(8,128)S(1)} %get-tuple-element.40), channel_id=1, source_target_pairs={{0,8},{8,16},{16,24},{24,0},{1,9},{9,17},{17,25},{25,1},{2,10},{10... | collective-permute-start | bytes 196616 | tf_op jit(solution)/shard_map/ppermute | solution.py:274
  49.3 6.7 %collective-permute-start.6 = (f32[1,128,128]{2,1,0:T(8,128)S(1)}, f32[1,128,128]{2,1,0:T(8,128)S(1)}, u32[]{:S(2)}, u32[]{:S(2)}) collective-permute-start(f32[1,128,128]{2,1,0:T(8,128)S(1)} %get-tuple-element.41), channel_id=1, source_target_pairs={{8,0},{16,8},{24,16},{0,24},{9,1},{17,9},{25,17},{1,25},{10,2},{18... | collective-permute-start | bytes 196616 | tf_op jit(solution)/shard_map/ppermute | solution.py:275
  51.3 4.7 %collective-permute-start.9 = (f32[2,4,8,128]{3,2,1,0:T(8,128)S(1)}, f32[2,4,8,128]{3,2,1,0:T(8,128)S(1)}, u32[]{:S(2)}, u32[]{:S(2)}) collective-permute-start(f32[2,4,8,128]{3,2,1,0:T(8,128)S(1)} %get-tuple-element.44), channel_id=1, source_target_pairs={{0,1},{1,0},{2,3},{3,2},{4,5},{5,4},{6,7},{7,6},{8,9},{9,8},{10,11... | collective-permute-start | bytes 98312 | tf_op jit(solution)/shard_map/ppermute | solution.py:279
  52.8 3.2 %collective-permute-start.7 = (f32[32,128]{1,0:T(8,128)S(1)}, f32[32,128]{1,0:T(8,128)S(1)}, u32[]{:S(2)}, u32[]{:S(2)}) collective-permute-start(f32[32,128]{1,0:T(8,128)S(1)} %get-tuple-element.42), channel_id=1, source_target_pairs={{0,2},{2,4},{4,6},{6,0},{1,3},{3,5},{5,7},{7,1},{8,10},{10,12},{12... | collective-permute-start | bytes 49160 | tf_op jit(solution)/shard_map/ppermute | solution.py:276
  52.8 3.2 %collective-permute-start.8 = (f32[32,128]{1,0:T(8,128)S(1)}, f32[32,128]{1,0:T(8,128)S(1)}, u32[]{:S(2)}, u32[]{:S(2)}) collective-permute-start(f32[32,128]{1,0:T(8,128)S(1)} %get-tuple-element.43), channel_id=1, source_target_pairs={{2,0},{4,2},{6,4},{0,6},{3,1},{5,3},{7,5},{1,7},{10,8},{12,10},{14... | collective-permute-start | bytes 49160 | tf_op jit(solution)/shard_map/ppermute | solution.py:277
  62.4 8.1 %collective-permute-start.10 = (f32[1,128,128]{2,1,0:T(8,128)S(1)}, f32[1,128,128]{2,1,0:T(8,128)S(1)}, u32[]{:S(2)}, u32[]{:S(2)}) collective-permute-start(f32[1,128,128]{2,1,0:T(8,128)S(1)} %get-tuple-element.46), channel_id=1, source_target_pairs={{0,8},{8,16},{16,24},{24,0},{1,9},{9,17},{17,25},{25,1},{2,10},{10... | collective-permute-start | bytes 196616 | tf_op jit(solution)/shard_map/ppermute | solution.py:274
  62.5 8.0 %collective-permute-start.11 = (f32[1,128,128]{2,1,0:T(8,128)S(1)}, f32[1,128,128]{2,1,0:T(8,128)S(1)}, u32[]{:S(2)}, u32[]{:S(2)}) collective-permute-start(f32[1,128,128]{2,1,0:T(8,128)S(1)} %get-tuple-element.47), channel_id=1, source_target_pairs={{8,0},{16,8},{24,16},{0,24},{9,1},{17,9},{25,17},{1,25},{10,2},{18... | collective-permute-start | bytes 196616 | tf_op jit(solution)/shard_map/ppermute | solution.py:275
  66.2 4.2 %collective-permute-start.14 = (f32[2,4,8,128]{3,2,1,0:T(8,128)S(1)}, f32[2,4,8,128]{3,2,1,0:T(8,128)S(1)}, u32[]{:S(2)}, u32[]{:S(2)}) collective-permute-start(f32[2,4,8,128]{3,2,1,0:T(8,128)S(1)} %get-tuple-element.50), channel_id=1, source_target_pairs={{0,1},{1,0},{2,3},{3,2},{4,5},{5,4},{6,7},{7,6},{8,9},{9,8},{10,11... | collective-permute-start | bytes 98312 | tf_op jit(solution)/shard_map/ppermute | solution.py:279
  67.0 3.2 %collective-permute-start.12 = (f32[32,128]{1,0:T(8,128)S(1)}, f32[32,128]{1,0:T(8,128)S(1)}, u32[]{:S(2)}, u32[]{:S(2)}) collective-permute-start(f32[32,128]{1,0:T(8,128)S(1)} %get-tuple-element.48), channel_id=1, source_target_pairs={{0,2},{2,4},{4,6},{6,0},{1,3},{3,5},{5,7},{7,1},{8,10},{10,12},{12... | collective-permute-start | bytes 49160 | tf_op jit(solution)/shard_map/ppermute | solution.py:276
  67.5 2.6 %collective-permute-start.13 = (f32[32,128]{1,0:T(8,128)S(1)}, f32[32,128]{1,0:T(8,128)S(1)}, u32[]{:S(2)}, u32[]{:S(2)}) collective-permute-start(f32[32,128]{1,0:T(8,128)S(1)} %get-tuple-element.49), channel_id=1, source_target_pairs={{2,0},{4,2},{6,4},{0,6},{3,1},{5,3},{7,5},{1,7},{10,8},{12,10},{14... | collective-permute-start | bytes 49160 | tf_op jit(solution)/shard_map/ppermute | solution.py:277
  70.5 13.0 %copy-start.8 = (s32[2048,8]{0,1:T(8,128)S(1)}, s32[2048,8]{0,1:T(8,128)}, u32[]{:S(2)}) copy-start(s32[2048,8]{0,1:T(8,128)} %param.17) | copy-start | bytes 196612
  70.5 13.0 %copy-start.9 = (f32[3,2048]{1,0:T(4,128)S(1)}, f32[3,2048]{1,0:T(4,128)}, u32[]{:S(2)}) copy-start(f32[3,2048]{1,0:T(4,128)} %param.15) | copy-start | bytes 73732
  76.8 8.1 %collective-permute-start.15 = (f32[1,128,128]{2,1,0:T(8,128)S(1)}, f32[1,128,128]{2,1,0:T(8,128)S(1)}, u32[]{:S(2)}, u32[]{:S(2)}) collective-permute-start(f32[1,128,128]{2,1,0:T(8,128)S(1)} %get-tuple-element.52), channel_id=1, source_target_pairs={{0,8},{8,16},{16,24},{24,0},{1,9},{9,17},{17,25},{25,1},{2,10},{10... | collective-permute-start | bytes 196616 | tf_op jit(solution)/shard_map/ppermute | solution.py:274
  76.9 8.0 %collective-permute-start.16 = (f32[1,128,128]{2,1,0:T(8,128)S(1)}, f32[1,128,128]{2,1,0:T(8,128)S(1)}, u32[]{:S(2)}, u32[]{:S(2)}) collective-permute-start(f32[1,128,128]{2,1,0:T(8,128)S(1)} %get-tuple-element.53), channel_id=1, source_target_pairs={{8,0},{16,8},{24,16},{0,24},{9,1},{17,9},{25,17},{1,25},{10,2},{18... | collective-permute-start | bytes 196616 | tf_op jit(solution)/shard_map/ppermute | solution.py:275
  80.7 4.2 %collective-permute-start.19 = (f32[2,4,8,128]{3,2,1,0:T(8,128)S(1)}, f32[2,4,8,128]{3,2,1,0:T(8,128)S(1)}, u32[]{:S(2)}, u32[]{:S(2)}) collective-permute-start(f32[2,4,8,128]{3,2,1,0:T(8,128)S(1)} %get-tuple-element.56), channel_id=1, source_target_pairs={{0,1},{1,0},{2,3},{3,2},{4,5},{5,4},{6,7},{7,6},{8,9},{9,8},{10,11... | collective-permute-start | bytes 98312 | tf_op jit(solution)/shard_map/ppermute | solution.py:279
  81.7 3.2 %collective-permute-start.17 = (f32[32,128]{1,0:T(8,128)S(1)}, f32[32,128]{1,0:T(8,128)S(1)}, u32[]{:S(2)}, u32[]{:S(2)}) collective-permute-start(f32[32,128]{1,0:T(8,128)S(1)} %get-tuple-element.54), channel_id=1, source_target_pairs={{0,2},{2,4},{4,6},{6,0},{1,3},{3,5},{5,7},{7,1},{8,10},{10,12},{12... | collective-permute-start | bytes 49160 | tf_op jit(solution)/shard_map/ppermute | solution.py:276
  82.4 2.5 %collective-permute-start.18 = (f32[32,128]{1,0:T(8,128)S(1)}, f32[32,128]{1,0:T(8,128)S(1)}, u32[]{:S(2)}, u32[]{:S(2)}) collective-permute-start(f32[32,128]{1,0:T(8,128)S(1)} %get-tuple-element.55), channel_id=1, source_target_pairs={{2,0},{4,2},{6,4},{0,6},{3,1},{5,3},{7,5},{1,7},{10,8},{12,10},{14... | collective-permute-start | bytes 49160 | tf_op jit(solution)/shard_map/ppermute | solution.py:277
